TPU v7x, 256 devices: a whole 4x4x8 slice. The times are simulated.
256 devices in a mesh: depth: 16 (over z, core), freq: 16 (over x, y).
Axes of the slice: x: 4, y: 4, z: 8, core: 2. Of those that a mesh axis runs over, the one named last changes fastest.
Arguments:
- fields_top: bfloat16 [16, 2, 16, 2, 384, 384], P('depth', None, 'freq'), may hold values from -6 to 6
- surface: bfloat16 [2, 2, 16, 2, 384, 384], P(None, None, 'freq'), may hold values from -6 to 6
- up_state: bfloat16 [16, 16, 2, 384, 384], P('depth', 'freq'), may hold values from -6 to 6
- angular_freq: float32 [16], P('freq'), may hold values from 0.5 to 2.5
- class_slowness: float32 [8], replicated, may hold values from 0.6 to 1.3
- velocity_class: int32 [16, 12, 12], P('depth'), may hold values from 0 to 7
- slowness_detail: float32 [16, 384, 384], P('depth'), may hold values from 0.5 to 1.5
Outputs:
- reflectivity: bfloat16 [16, 384, 384], P('depth', 'freq')
- up_out: bfloat16 [16, 16, 2, 384, 384], P('depth', 'freq')
All inputs are finite; a program needn't handle non-finite values.
Results may differ from a plain program's by a relative error of at most 0.023.
Values may be sent and summed in bfloat16 or wider, within the bound.
No kernel may reach another device: no remote copies, remote signals or barrier semaphores. Data moves between devices by JAX's collectives and lax.ppermute only.
A program may use at most 64 MiB of HBM per device.

v0:
```python
from functools import partial

import jax
import jax.numpy as jnp
import ml_dtypes
import numpy as np
from jax import lax
from jax.experimental import pallas as pl
from jax.experimental.pallas import tpu as pltpu
from jax.sharding import PartitionSpec as P

TICKS = 3
BLOCK = 32
DEPTH_STEP = 1.0
EPSILON = 1e-06
F32 = jnp.float32
BF16 = jnp.bfloat16


def transform_tables(lateral):
    half = lateral // 2
    place = np.arange(lateral)
    wave = np.where(place <= half, place, place - half)
    angles = (place[:, None] * wave[None, :] % lateral) * (2.0 * np.pi / lateral)
    basis = np.where(place[None, :] <= half, np.cos(angles), np.sin(angles))
    basis = basis.astype(np.float32).astype(ml_dtypes.bfloat16)
    return basis, np.ascontiguousarray(basis.T)


def sincos(x):
    turns = jnp.round(x * (2.0 / np.pi))
    r = x - turns * 1.5703125
    r = r - turns * 4.837512969970703125e-4
    r = r - turns * 7.54978995489188216e-8
    z = r * r
    sin_r = r + r * z * (-1.6666654611e-1 + z * (8.3321608736e-3 + z * -1.9515295891e-4))
    cos_r = 1.0 - 0.5 * z + z * z * (4.166664568298827e-2 + z * (-1.388731625493765e-3 + z * 2.443315711809948e-5))
    quarter = turns.astype(jnp.int32)
    swap = (quarter & 1) == 1
    sin_x = jnp.where(swap, cos_r, sin_r)
    cos_x = jnp.where(swap, sin_r, cos_r)
    sin_x = jnp.where((quarter & 2) == 2, -sin_x, sin_x)
    cos_x = jnp.where(((quarter + 1) & 2) == 2, -cos_x, cos_x)
    return sin_x, cos_x


def phases_body(classes, scalars, detail, phase_re, phase_im, lens_re, lens_im, kinds_of):
    lateral = detail.shape[0]
    blocks = lateral // BLOCK
    half = lateral // 2
    step = 2.0 * np.pi / lateral
    lane_block = lax.broadcasted_iota(jnp.int32, (1, lateral), 1) // BLOCK

    def axis_terms(shape, dim, offset):
        place = lax.broadcasted_iota(jnp.int32, shape, dim) + offset
        wave = jnp.where(place <= half, place, place - half)
        kappa = wave.astype(F32) * step
        weight = jnp.where((wave == 0) | (wave == half), 1.0, 2.0)
        return kappa * kappa, weight

    lane_sq, lane_weight = axis_terms((1, lateral), 1, 0)
    for i in range(blocks):
        kinds_of[i : i + 1, :] = classes[i]
    kinds = kinds_of[...]
    slow = jnp.zeros(kinds.shape, F32)
    count = scalars.shape[1] - 1
    for kind in range(count):
        slow = jnp.where(kinds == kind, scalars[0:1, kind : kind + 1], slow)
    w = scalars[0:1, count : count + 1]
    spread = jnp.zeros((blocks, lateral), F32)
    for j in range(blocks):
        spread = jnp.where(lane_block == j, slow[:, j : j + 1], spread)
    total = jnp.zeros((8, lateral), F32)
    for i in range(blocks):
        cells = spread[i : i + 1, :] * detail[i * BLOCK : (i + 1) * BLOCK, :]
        lens_re[i * BLOCK : (i + 1) * BLOCK, :] = cells
        total = total + cells.reshape(BLOCK // 8, 8, lateral).sum(axis=0)
    mean = jnp.sum(jnp.sum(total, axis=0, keepdims=True), axis=1, keepdims=True) / (lateral * lateral)
    square = (w * mean) * (w * mean)
    scale = w * DEPTH_STEP

    def phases(start, rows):
        row_sq, row_weight = axis_terms((rows, 1), 0, start)
        vertical = square - (row_sq + lane_sq)
        root = jnp.sqrt(jnp.abs(vertical)) * DEPTH_STEP
        decay = jnp.where(vertical < 0.0, jnp.exp(-root), 1.0)
        decay = decay * (row_weight * lane_weight / (lateral * lateral))
        travel_sin, travel_cos = sincos(jnp.where(vertical > 0.0, root, 0.0))
        return decay * travel_cos, decay * travel_sin

    rows = 32

    def lens(index, carry):
        here = pl.ds(pl.multiple_of(index * rows, rows), rows)
        lens_sin, lens_cos = sincos(scale * (lens_re[here, :] - mean))
        lens_re[here, :] = lens_cos
        lens_im[here, :] = lens_sin
        return carry

    lax.fori_loop(0, lateral // rows, lens, 0, unroll=2)

    def spectral(index, carry):
        start = pl.multiple_of(index * rows, rows)
        real, imag = phases(start, rows)
        for first in (0, half):
            here = pl.ds(pl.multiple_of(start + first, rows), rows)
            phase_re[here, :] = real
            phase_im[here, :] = imag
        return carry

    lax.fori_loop(0, half // rows, spectral, 0, unroll=2)
    phase_re[half : half + 8, :], phase_im[half : half + 8, :] = phases(half, 8)


def step_core(start, basis, basis_t, phase_re, phase_im, lens_re, lens_im, wide, tall, write):
    n = basis.shape[0]
    first = jnp.dot(start, basis[...], preferred_element_type=F32).astype(BF16)
    wide[:, :n] = first[:n]
    wide[:, n:] = first[n:]
    spectrum = jnp.dot(basis_t[...], wide[...], preferred_element_type=F32)
    spec_re, spec_im = spectrum[:, :n], spectrum[:, n:]
    wide[:, :n] = (spec_re * phase_re[...] - spec_im * phase_im[...]).astype(BF16)
    wide[:, n:] = (spec_re * phase_im[...] + spec_im * phase_re[...]).astype(BF16)
    back = jnp.dot(basis[...], wide[...], preferred_element_type=F32).astype(BF16)
    tall[:n, :] = back[:, :n]
    tall[n:, :] = back[:, n:]
    space = jnp.dot(tall[...], basis_t[...], preferred_element_type=F32)
    space_re, space_im = space[:n], space[n:]
    write(
        (space_re * lens_re[...] - space_im * lens_im[...]).astype(BF16),
        (space_re * lens_im[...] + space_im * lens_re[...]).astype(BF16),
    )


def entering(arrived, surface, tick, kind, tall):
    n = arrived.shape[-1]

    @pl.when(lax.axis_index("depth") == 0)
    def _():
        tall[...] = surface[tick - 1, kind, 0].reshape(2 * n, n)

    @pl.when(lax.axis_index("depth") != 0)
    def _():
        tall[...] = arrived[...].reshape(2 * n, n)

    return tall[...]


def put(out):
    def write(real, imag):
        out[0] = real
        out[1] = imag

    return write


TABLES = 6


def first_body(start, *refs):
    tables, (out, wide, tall) = refs[:TABLES], refs[TABLES:]
    n = start.shape[-1]
    step_core(start[0, 0, 0].reshape(2 * n, n), *tables, wide, tall, put(out))


def later_body(tick, arrived, surface, *refs):
    tables, (out, wide, tall) = refs[:TABLES], refs[TABLES:]
    step_core(entering(arrived, surface, tick, 0, tall), *tables, wide, tall, put(out))


def add_terms(source, receiver, image, illum):
    s_re, s_im = source[0].astype(F32), source[1].astype(F32)
    r_re, r_im = receiver[0].astype(F32), receiver[1].astype(F32)
    return image + (s_re * r_re + s_im * r_im), illum + (s_re * s_re + s_im * s_im)


def pieces(value, rows):
    high = value.astype(BF16).astype(F32)
    middle = (value - high).astype(BF16).astype(F32)
    low = value - high - middle
    row = lax.broadcasted_iota(jnp.int32, (rows, 128), 0)
    parts = jnp.where(row == 0, high, jnp.where(row == 1, middle, jnp.where(row == 2, low, 0.0)))
    return parts.astype(BF16)


def first_image_body(start, source, *refs):
    tables, (out, image, illum, wide, tall) = refs[:TABLES], refs[TABLES:]
    n = start.shape[-1]
    step_core(start[0, 1, 0].reshape(2 * n, n), *tables, wide, tall, put(out))
    image[...], illum[...] = add_terms(source, out, 0.0, 0.0)


def later_image_body(tick, arrived, surface, source, image_in, illum_in, *refs):
    tables, (out, image, illum, wide, tall) = refs[:TABLES], refs[TABLES:]
    step_core(entering(arrived, surface, tick, 1, tall), *tables, wide, tall, put(out))
    image[...], illum[...] = add_terms(source, out, image_in[...], illum_in[...])


def last_image_body(tick, rising, arrived, surface, source, image_in, illum_in, *refs):
    tables, (parcel, wide, tall, out) = refs[:TABLES], refs[TABLES:]
    peers = parcel.shape[0]
    n = illum_in.shape[0]
    rows = n // peers
    lit = 3 * rows
    total = jnp.zeros((rows, n), F32)
    for peer in range(peers):
        here = slice(peer * rows, (peer + 1) * rows)
        s_re, s_im = source[0, here, :].astype(F32), source[1, here, :].astype(F32)
        illum = illum_in[here, :] + (s_re * s_re + s_im * s_im)
        total = total + illum
        small = illum.astype(BF16)
        for lane in range(3):
            there = slice(lit + lane * rows, lit + (lane + 1) * rows)
            parcel[peer, there, :] = small[:, lane * 128 : (lane + 1) * 128]
    extra = pieces(jnp.sum(total), 16)
    for peer in range(peers):
        parcel[peer, 2 * lit : 2 * lit + 16, :] = extra
    step_core(entering(arrived, surface, tick, 1, tall), *tables, wide, tall, put(out))
    for peer in range(peers):
        here = slice(peer * rows, (peer + 1) * rows)
        image = image_in[here, :]
        for part in range(2):
            image = image + source[part, here, :].astype(F32) * out[part, here, :].astype(F32)
        small = image.astype(BF16)
        for lane in range(3):
            parcel[peer, lane * rows : (lane + 1) * rows, :] = small[:, lane * 128 : (lane + 1) * 128]


def balance_body(parcel, out):
    peers, height, lanes = parcel.shape
    lit = (height - 16) // 2
    cells = lit * lanes * peers
    sums = parcel[0].astype(F32)
    for peer in range(1, peers):
        sums = sums + parcel[peer].astype(F32)
    image, illum = sums[:lit], sums[lit : 2 * lit]
    damping = jnp.sum(sums[2 * lit :, 0:1]) / cells
    balanced = image / (illum + damping)
    small = balanced.astype(BF16)
    extra = pieces(jnp.sum(balanced * balanced), 8)
    for peer in range(peers):
        out[peer, 0:lit, :] = small
        out[peer, lit : lit + 8, :] = extra


def upward_body(parcel, rising, source, *refs):
    tables, (part, out, wide, tall) = refs[:TABLES], refs[TABLES:]
    peers, _, lanes = parcel.shape
    n = source.shape[-1]
    rows = n // peers
    square = jnp.zeros((8, lanes), F32)
    for peer in range(peers):
        square = square + parcel[peer, 3 * rows : 3 * rows + 8, :].astype(F32)
    scale = lax.rsqrt(jnp.sum(square[:, 0:1]) / (n * n) + EPSILON)
    own = (parcel[pl.ds(lax.axis_index("freq"), 1)][0].astype(F32) * scale).astype(BF16)
    for lane in range(3):
        part[:, lane * lanes : (lane + 1) * lanes] = own[lane * rows : (lane + 1) * rows]
    for peer in range(peers):
        here = slice(peer * rows, (peer + 1) * rows)
        for lane in range(3):
            there = slice(lane * lanes, (lane + 1) * lanes)
            reflect = parcel[peer, lane * rows : (lane + 1) * rows, :].astype(F32) * scale
            reflect = reflect.astype(BF16).astype(F32)
            for half in range(2):
                lifted = rising[half, here, there].astype(F32) + reflect * source[half, here, there].astype(F32)
                tall[half * n + peer * rows : half * n + (peer + 1) * rows, there] = lifted.astype(BF16)
    step_core(tall[...], *tables, wide, tall, put(out))


def passed_along(block, axis, distance):
    devices = range(lax.axis_size(axis))
    route = [(i - distance, i) for i in devices if i - distance in devices]
    return lax.ppermute(block, axis, route)


def exchanged(parcel):
    return lax.all_to_all(parcel, "freq", split_axis=0, concat_axis=0, tiled=True)


def per_device(
    fields_top, surface, up_state, angular_freq, class_slowness, velocity_class, slowness_detail
):
    n = fields_top.shape[-1]
    peers = lax.axis_size("freq")
    vmem = pl.BlockSpec(memory_space=pltpu.VMEM)
    field = jax.ShapeDtypeStruct((2, n, n), BF16)
    cells = jax.ShapeDtypeStruct((n, n), F32)
    work = [pltpu.VMEM((n, 2 * n), BF16), pltpu.VMEM((2 * n, n), BF16)]
    cost = pl.CostEstimate(flops=2 * 4 * 2 * n**3, transcendentals=0, bytes_accessed=8 * n * n)

    def call(body, in_specs, out_shape, scratch):
        return pl.pallas_call(
            body,
            in_specs=in_specs,
            out_specs=jax.tree.map(lambda _: vmem, out_shape),
            out_shape=out_shape,
            scratch_shapes=scratch,
            cost_estimate=cost,
            compiler_params=pltpu.CompilerParams(vmem_limit_bytes=14 << 20),
        )

    rows = n // peers
    lit = rows * n // 128
    basis, basis_t = (jnp.asarray(table) for table in transform_tables(n))
    scalars = jnp.concatenate([class_slowness, angular_freq])[None]
    kinds = velocity_class.transpose(1, 0, 2)
    scratch = [pltpu.VMEM((kinds.shape[0], kinds.shape[2]), jnp.int32)]
    phases = call(phases_body, [vmem] * 3, [cells] * 4, scratch)(kinds, scalars, slowness_detail[0])
    tables = (basis, basis_t, *phases)
    source = call(first_body, [vmem] * (1 + TABLES), field, work)(fields_top, *tables)
    sent_source = passed_along(source, "depth", 1)
    receiver, image, illum = call(
        first_image_body, [vmem] * (2 + TABLES), [field, cells, cells], work
    )(fields_top, source, *tables)
    rising = passed_along(up_state[0, 0], "depth", -1)
    for tick in range(1, TICKS):
        sent_receiver = passed_along(receiver, "depth", 1)
        source = call(
            partial(later_body, tick), [vmem] * (2 + TABLES), field, work
        )(sent_source, surface, *tables)
        args = (sent_receiver, surface, source, image, illum, *tables)
        specs = [vmem] * (5 + TABLES)
        if tick + 1 < TICKS:
            sent_source = passed_along(source, "depth", 1)
            receiver, image, illum = call(
                partial(later_image_body, tick), specs, [field, cells, cells], work
            )(*args)
        else:
            parcel = jax.ShapeDtypeStruct((peers, 2 * lit + 16, 128), BF16)
            parcel = call(
                partial(last_image_body, tick),
                [vmem] + specs,
                parcel,
                work + [pltpu.VMEM((2, n, n), BF16)],
            )(rising, *args)
    balanced = jax.ShapeDtypeStruct((peers, lit + 8, 128), BF16)
    balanced = call(balance_body, [vmem], balanced, [])(exchanged(parcel))
    part, risen = call(
        upward_body, [vmem] * (3 + TABLES), [jax.ShapeDtypeStruct((rows, n), BF16), field], work
    )(exchanged(balanced), rising, source, *tables)
    return (part[None], risen[None, None])


def solution(mesh):
    return jax.shard_map(
        per_device,
        mesh=mesh,
        in_specs=(
            P("depth", None, "freq", None, None, None),
            P(None, None, "freq", None, None, None),
            P("depth", "freq", None, None, None),
            P("freq"),
            P(),
            P("depth", None, None),
            P("depth", None, None),
        ),
        out_specs=(P("depth", "freq", None), P("depth", "freq", None, None, None)),
        check_vma=False,
    )
```

profile of v0, /device:TPU:96, one launch (start us, length us, event | category | flops | bytes accessed | tf_op | source)
XLA Modules:
  0.0 79.2 jit_solution(8404661389696841554)
XLA Ops:
  0.6 0.0 copy-start.1
  0.6 0.0 copy-start.2
  0.7 0.0 copy-start.3
  1.4 0.7 maximum_bitcast_fusion.scalars
  2.2 0.0 copy-start.4
  2.2 1.1 %copy-done.4 = f32[1,384,384]{2,1,0:T(8,128)S(1)} copy-done((f32[1,384,384]{2,1,0:T(8,128)S(1)}, f32[1,384,384]{2,1,0:T(8,128)}, u32[]{:S(2)}) %copy-start.4) | copy-done | bytes 589848
  3.2 0.0 copy-start.5
  3.2 0.7 copy-done.5
  3.9 2.5 %shard_map.104 = (f32[384,384]{1,0:T(8,128)S(1)}, f32[384,384]{1,0:T(8,128)S(1)}, f32[384,384]{1,0:T(8,128)S(1)}, f32[384,384]{1,0:T(8,128)S(1)}) custom-call(s32[12,1,12]{2,1,0:T(1,128)S(1)} %bitcast.8, f32[1,9]{1,0:T(1,128)S(1)} %maximum_bitcast_fusion.scalars, f32[384,384]{1,0:T(8,128)S(1)} %bitcast.7), custom_call_target="tpu_custom_call" | custom-call | flops 905969664 | bytes 1179648 | tf_op jit(solution)/shard_map/pallas_call | solution.py:308
  6.4 0.0 copy-done.1
  6.4 0.0 copy-done.2
  6.5 0.0 copy-done.3
  6.5 1.9 %shard_map.105.source = bf16[2,384,384]{2,1,0:T(8,128)(2,1)S(1)} custom-call(bf16[1,2,1,2,384,384]{5,4,3,2,1,0:T(8,128)(2,1)S(1)} %copy-done.3, bf16[384,384]{1,0:T(8,128)(2,1)S(1)} %copy-done.1, bf16[384,384]{1,0:T(8,128)(2,1)S(1)} %copy-done.2, f32[384,384]{1,0:T(8,128)S(1)} %get-tuple-element.14.refs_2_, f32[384,384]{1,0:T(8,128)S(1)} %get-tuple-element.15.refs_3_, ...), custom_call_target="tpu_custom_call" | custom-call | flops 905969664 | bytes 1179648 | tf_op jit(solution)/shard_map/pallas_call | solution.py:310
  8.4 0.0 copy-start.6
  8.4 0.0 copy-start
  8.4 2.2 %collective-permute-start.2 = (bf16[2,384,384]{2,1,0:T(8,128)(2,1)S(1)}, bf16[2,384,384]{2,1,0:T(8,128)(2,1)S(1)}, u32[]{:S(2)}, u32[]{:S(2)}) collective-permute-start(bf16[2,384,384]{2,1,0:T(8,128)(2,1)S(1)} %shard_map.105.source), channel_id=1, source_target_pairs={{0,16},{16,32},{32,48},{48,64},{64,80},{80,96},{96,112},{112,128},... | collective-permute-start | bytes 1769480 | tf_op jit(solution)/shard_map/ppermute | solution.py:273
  10.6 2.2 %shard_map.106 = (bf16[2,384,384]{2,1,0:T(8,128)(2,1)S(1)}, f32[384,384]{1,0:T(8,128)S(1)}, f32[384,384]{1,0:T(8,128)S(1)}) custom-call(bf16[1,2,1,2,384,384]{5,4,3,2,1,0:T(8,128)(2,1)S(1)} %copy-done.3, bf16[2,384,384]{2,1,0:T(8,128)(2,1)S(1)} %shard_map.105.source, bf16[384,384]{1,0:T(8,128)(2,1)S(1)} %copy-done.1, bf16[384,384]{1,0:T(8,128)(2,1)S(1)} %copy-done.2, ...), custom_call_target="tpu_custom_call" | custom-call | flops 905969664 | bytes 1179648 | tf_op jit(solution)/shard_map/pallas_call | solution.py:312
  12.8 5.1 %collective-permute-start.1 = (bf16[2,384,384]{2,1,0:T(8,128)(2,1)S(1)}, bf16[2,384,384]{2,1,0:T(8,128)(2,1)S(1)}, u32[]{:S(2)}, u32[]{:S(2)}) collective-permute-start(bf16[2,384,384]{2,1,0:T(8,128)(2,1)S(1)} %get-tuple-element.18), channel_id=1, source_target_pairs={{0,16},{16,32},{32,48},{48,64},{64,80},{80,96},{96,112},{112,128},... | collective-permute-start | bytes 1769480 | tf_op jit(solution)/shard_map/ppermute | solution.py:273
  17.9 0.0 copy-done.6
  18.0 1.9 %collective-permute-start = (bf16[2,384,384]{2,1,0:T(8,128)(2,1)S(1)}, bf16[2,384,384]{2,1,0:T(8,128)(2,1)S(1)}, u32[]{:S(2)}, u32[]{:S(2)}) collective-permute-start(bf16[2,384,384]{2,1,0:T(8,128)(2,1)S(1)} %bitcast.9), channel_id=1, source_target_pairs={{16,0},{32,16},{48,32},{64,48},{80,64},{96,80},{112,96},{128,112},... | collective-permute-start | bytes 1769480 | tf_op jit(solution)/shard_map/ppermute | solution.py:273
  19.9 0.0 collective-permute-done.2.arrived
  19.9 0.0 copy-done
  19.9 2.0 %shard_map.107.source = bf16[2,384,384]{2,1,0:T(8,128)(2,1)S(1)} custom-call(bf16[2,384,384]{2,1,0:T(8,128)(2,1)S(1)} %collective-permute-done.2.arrived, bf16[2,2,1,2,384,384]{5,4,3,2,1,0:T(8,128)(2,1)S(1)} %copy-done, bf16[384,384]{1,0:T(8,128)(2,1)S(1)} %copy-done.1, bf16[384,384]{1,0:T(8,128)(2,1)S(1)} %copy-done.2, ...), custom_call_target="tpu_custom_call" | custom-call | flops 905969664 | bytes 1179648 | tf_op jit(solution)/shard_map/pallas_call | solution.py:318
  21.9 2.7 %collective-permute-start.4 = (bf16[2,384,384]{2,1,0:T(8,128)(2,1)S(1)}, bf16[2,384,384]{2,1,0:T(8,128)(2,1)S(1)}, u32[]{:S(2)}, u32[]{:S(2)}) collective-permute-start(bf16[2,384,384]{2,1,0:T(8,128)(2,1)S(1)} %shard_map.107.source), channel_id=1, source_target_pairs={{0,16},{16,32},{32,48},{48,64},{64,80},{80,96},{96,112},{112,128},... | collective-permute-start | bytes 1769480 | tf_op jit(solution)/shard_map/ppermute | solution.py:273
  24.6 1.6 %collective-permute-done.1.arrived = bf16[2,384,384]{2,1,0:T(8,128)(2,1)S(1)} collective-permute-done((bf16[2,384,384]{2,1,0:T(8,128)(2,1)S(1)}, bf16[2,384,384]{2,1,0:T(8,128)(2,1)S(1)}, u32[]{:S(2)}, u32[]{:S(2)}) %collective-permute-start.1) | collective-permute-done | bytes 589856 | tf_op jit(solution)/shard_map/ppermute | solution.py:273
  26.2 2.2 %shard_map.108 = (bf16[2,384,384]{2,1,0:T(8,128)(2,1)S(1)}, f32[384,384]{1,0:T(8,128)S(1)}, f32[384,384]{1,0:T(8,128)S(1)}) custom-call(bf16[2,384,384]{2,1,0:T(8,128)(2,1)S(1)} %collective-permute-done.1.arrived, bf16[2,2,1,2,384,384]{5,4,3,2,1,0:T(8,128)(2,1)S(1)} %copy-done, bf16[2,384,384]{2,1,0:T(8,128)(2,1)S(1)} %shard_map.107.source, ...), custom_call_target="tpu_custom_call" | custom-call | flops 905969664 | bytes 1179648 | tf_op jit(solution)/shard_map/pallas_call | solution.py:325
  28.5 4.0 %collective-permute-start.3 = (bf16[2,384,384]{2,1,0:T(8,128)(2,1)S(1)}, bf16[2,384,384]{2,1,0:T(8,128)(2,1)S(1)}, u32[]{:S(2)}, u32[]{:S(2)}) collective-permute-start(bf16[2,384,384]{2,1,0:T(8,128)(2,1)S(1)} %get-tuple-element.21), channel_id=1, source_target_pairs={{0,16},{16,32},{32,48},{48,64},{64,80},{80,96},{96,112},{112,128},... | collective-permute-start | bytes 1769480 | tf_op jit(solution)/shard_map/ppermute | solution.py:273
  32.5 0.6 collective-permute-done.4.arrived
  33.1 2.0 %shard_map.109.source = bf16[2,384,384]{2,1,0:T(8,128)(2,1)S(1)} custom-call(bf16[2,384,384]{2,1,0:T(8,128)(2,1)S(1)} %collective-permute-done.4.arrived, bf16[2,2,1,2,384,384]{5,4,3,2,1,0:T(8,128)(2,1)S(1)} %copy-done, bf16[384,384]{1,0:T(8,128)(2,1)S(1)} %copy-done.1, bf16[384,384]{1,0:T(8,128)(2,1)S(1)} %copy-done.2, ...), custom_call_target="tpu_custom_call" | custom-call | flops 905969664 | bytes 1179648 | tf_op jit(solution)/shard_map/pallas_call | solution.py:318
  35.1 0.0 collective-permute-done.rising
  35.1 4.5 %collective-permute-done.3.arrived = bf16[2,384,384]{2,1,0:T(8,128)(2,1)S(1)} collective-permute-done((bf16[2,384,384]{2,1,0:T(8,128)(2,1)S(1)}, bf16[2,384,384]{2,1,0:T(8,128)(2,1)S(1)}, u32[]{:S(2)}, u32[]{:S(2)}) %collective-permute-start.3) | collective-permute-done | bytes 589856 | tf_op jit(solution)/shard_map/ppermute | solution.py:273
  39.7 2.7 %shard_map.110 = bf16[16,160,128]{2,1,0:T(8,128)(2,1)S(1)} custom-call(bf16[2,384,384]{2,1,0:T(8,128)(2,1)S(1)} %collective-permute-done.rising, bf16[2,384,384]{2,1,0:T(8,128)(2,1)S(1)} %collective-permute-done.3.arrived, bf16[2,2,1,2,384,384]{5,4,3,2,1,0:T(8,128)(2,1)S(1)} %copy-done, bf16[2,384,384]{2,1,0:T(8,128)(2,1)S(1)} %shard_map.109.source, ...), custom_call_target="tpu_custom_call" | custom-call | flops 905969664 | bytes 1179648 | tf_op jit(solution)/shard_map/pallas_call | solution.py:330
  42.4 20.1 %all_to_all.10.parcel = bf16[16,160,128]{2,1,0:T(8,128)(2,1)S(1)} all-to-all(bf16[16,160,128]{2,1,0:T(8,128)(2,1)S(1)} %shard_map.110), channel_id=1, replica_groups=mesh['depth'=16,'freq'=16] {'freq'}, dimensions={0} | all-to-all | bytes 1310720 | tf_op jit(solution)/shard_map/all_to_all | solution.py:277
  62.4 0.3 shard_map.111
  62.7 13.5 %all_to_all.11.parcel = bf16[16,80,128]{2,1,0:T(8,128)(2,1)S(1)} all-to-all(bf16[16,80,128]{2,1,0:T(8,128)(2,1)S(1)} %shard_map.111), channel_id=1, replica_groups=mesh['depth'=16,'freq'=16] {'freq'}, dimensions={0} | all-to-all | bytes 655360 | tf_op jit(solution)/shard_map/all_to_all | solution.py:277
  76.2 3.0 %shard_map.112 = (bf16[24,384]{1,0:T(8,128)(2,1)}, bf16[2,384,384]{2,1,0:T(8,128)(2,1)}) custom-call(bf16[16,80,128]{2,1,0:T(8,128)(2,1)S(1)} %all_to_all.11.parcel, bf16[2,384,384]{2,1,0:T(8,128)(2,1)S(1)} %collective-permute-done.rising, bf16[2,384,384]{2,1,0:T(8,128)(2,1)S(1)} %shard_map.109.source, bf16[384,384]{1,0:T(8,128)(2,1)S(1)} %copy-done.1, ...), custom_call_target="tpu_custom_call" | custom-call | flops 905969664 | bytes 1179648 | tf_op jit(solution)/shard_map/pallas_call | solution.py:338
Async XLA Ops:
  0.6 5.8 %copy-start.1 = (bf16[384,384]{1,0:T(8,128)(2,1)S(1)}, bf16[384,384]{1,0:T(8,128)(2,1)}, u32[]{:S(2)}) copy-start(bf16[384,384]{1,0:T(8,128)(2,1)} %constant.4.clone.refs_0_) | copy-start | bytes 884740
  0.6 5.8 %copy-start.2 = (bf16[384,384]{1,0:T(8,128)(2,1)S(1)}, bf16[384,384]{1,0:T(8,128)(2,1)}, u32[]{:S(2)}) copy-start(bf16[384,384]{1,0:T(8,128)(2,1)} %constant.5.clone.refs_1_) | copy-start | bytes 884740
  0.7 5.8 %copy-start.3 = (bf16[1,2,1,2,384,384]{5,4,3,2,1,0:T(8,128)(2,1)S(1)}, bf16[1,2,1,2,384,384]{5,4,3,2,1,0:T(8,128)(2,1)}, u32[]{:S(2)}) copy-start(bf16[1,2,1,2,384,384]{5,4,3,2,1,0:T(8,128)(2,1)} %start.3) | copy-start | bytes 3538948
  2.2 1.1 %copy-start.4 = (f32[1,384,384]{2,1,0:T(8,128)S(1)}, f32[1,384,384]{2,1,0:T(8,128)}, u32[]{:S(2)}) copy-start(f32[1,384,384]{2,1,0:T(8,128)} %param.15) | copy-start | bytes 1769476
  3.2 0.7 copy-start.5
  8.4 9.5 %copy-start.6 = (bf16[1,1,2,384,384]{4,3,2,1,0:T(8,128)(2,1)S(1)}, bf16[1,1,2,384,384]{4,3,2,1,0:T(8,128)(2,1)}, u32[]{:S(2)}) copy-start(bf16[1,1,2,384,384]{4,3,2,1,0:T(8,128)(2,1)} %param.11) | copy-start | bytes 1769476
  8.4 11.5 %copy-start = (bf16[2,2,1,2,384,384]{5,4,3,2,1,0:T(8,128)(2,1)S(1)}, bf16[2,2,1,2,384,384]{5,4,3,2,1,0:T(8,128)(2,1)}, u32[]{:S(2)}) copy-start(bf16[2,2,1,2,384,384]{5,4,3,2,1,0:T(8,128)(2,1)} %surface.7) | copy-start | bytes 7077892
  8.4 11.5 %collective-permute-start.2 = (bf16[2,384,384]{2,1,0:T(8,128)(2,1)S(1)}, bf16[2,384,384]{2,1,0:T(8,128)(2,1)S(1)}, u32[]{:S(2)}, u32[]{:S(2)}) collective-permute-start(bf16[2,384,384]{2,1,0:T(8,128)(2,1)S(1)} %shard_map.105.source), channel_id=1, source_target_pairs={{0,16},{16,32},{32,48},{48,64},{64,80},{80,96},{96,112},{112,128},... | collective-permute-start | bytes 1769480 | tf_op jit(solution)/shard_map/ppermute | solution.py:273
  12.8 13.4 %collective-permute-start.1 = (bf16[2,384,384]{2,1,0:T(8,128)(2,1)S(1)}, bf16[2,384,384]{2,1,0:T(8,128)(2,1)S(1)}, u32[]{:S(2)}, u32[]{:S(2)}) collective-permute-start(bf16[2,384,384]{2,1,0:T(8,128)(2,1)S(1)} %get-tuple-element.18), channel_id=1, source_target_pairs={{0,16},{16,32},{32,48},{48,64},{64,80},{80,96},{96,112},{112,128},... | collective-permute-start | bytes 1769480 | tf_op jit(solution)/shard_map/ppermute | solution.py:273
  18.0 17.2 %collective-permute-start = (bf16[2,384,384]{2,1,0:T(8,128)(2,1)S(1)}, bf16[2,384,384]{2,1,0:T(8,128)(2,1)S(1)}, u32[]{:S(2)}, u32[]{:S(2)}) collective-permute-start(bf16[2,384,384]{2,1,0:T(8,128)(2,1)S(1)} %bitcast.9), channel_id=1, source_target_pairs={{16,0},{32,16},{48,32},{64,48},{80,64},{96,80},{112,96},{128,112},... | collective-permute-start | bytes 1769480 | tf_op jit(solution)/shard_map/ppermute | solution.py:273
  21.9 11.2 %collective-permute-start.4 = (bf16[2,384,384]{2,1,0:T(8,128)(2,1)S(1)}, bf16[2,384,384]{2,1,0:T(8,128)(2,1)S(1)}, u32[]{:S(2)}, u32[]{:S(2)}) collective-permute-start(bf16[2,384,384]{2,1,0:T(8,128)(2,1)S(1)} %shard_map.107.source), channel_id=1, source_target_pairs={{0,16},{16,32},{32,48},{48,64},{64,80},{80,96},{96,112},{112,128},... | collective-permute-start | bytes 1769480 | tf_op jit(solution)/shard_map/ppermute | solution.py:273
  28.5 11.2 %collective-permute-start.3 = (bf16[2,384,384]{2,1,0:T(8,128)(2,1)S(1)}, bf16[2,384,384]{2,1,0:T(8,128)(2,1)S(1)}, u32[]{:S(2)}, u32[]{:S(2)}) collective-permute-start(bf16[2,384,384]{2,1,0:T(8,128)(2,1)S(1)} %get-tuple-element.21), channel_id=1, source_target_pairs={{0,16},{16,32},{32,48},{48,64},{64,80},{80,96},{96,112},{112,128},... | collective-permute-start | bytes 1769480 | tf_op jit(solution)/shard_map/ppermute | solution.py:273
where the time goes:
time: 79.6 us; the launch traced here: 79.2 us
  blocking collectives  33.5 us (42%)
  Pallas kernels  18.8 us (24%)
  starting transfers between devices  15.9 us (20%)
  waiting for transfers between devices  6.85 us (9%)
  local copies, waits for them, and re-layouts  1.79 us (2%)
  between operations  1.58 us (2%)
    all_to_all x2, blocking collectives, exchanged(): lax.all_to_all(parcel, 'freq', split_axis=0, concat_axis=0, tiled=True)  33.5 us
    ppermute x5, starting transfers between devices, passed_along(): return lax.ppermute(block, axis, route)  15.9 us
    ppermute x5, waiting for transfers between devices, passed_along(): return lax.ppermute(block, axis, route)  6.85 us
    pallas_call x2, Pallas kernels, per_device(): call(partial(later_body, tick), [vmem] * (2 + TABLES), field, work)  4 us
    pallas_call x1, Pallas kernels, per_device(): call(upward_body, [vmem] * (3 + TABLES), [jax.ShapeDtypeStruct((rows, n),...  2.98 us
    pallas_call x1, Pallas kernels, per_device(): call(partial(last_image_body, tick), [vmem] + specs, parcel, work + [pltp...  2.66 us
    pallas_call x1, Pallas kernels, per_device(): call(phases_body, [vmem] * 3, [cells] * 4, scratch)  2.5 us
    pallas_call x1, Pallas kernels, per_device(): call(partial(later_image_body, tick), specs, [field, cells, cells], work)  2.25 us
  transfers between devices with their start and end apart: 5, of which 3 were waited for; matrix products, arithmetic and copies ran while one was open for 0% of the time, Pallas kernels for 11%

commit v1 on v0

--- a/solution.py
+++ b/solution.py
@@ -28,23 +28,35 @@
 
 
 def sincos(x):
-    turns = jnp.round(x * (2.0 / np.pi))
-    r = x - turns * 1.5703125
-    r = r - turns * 4.837512969970703125e-4
-    r = r - turns * 7.54978995489188216e-8
-    z = r * r
-    sin_r = r + r * z * (-1.6666654611e-1 + z * (8.3321608736e-3 + z * -1.9515295891e-4))
-    cos_r = 1.0 - 0.5 * z + z * z * (4.166664568298827e-2 + z * (-1.388731625493765e-3 + z * 2.443315711809948e-5))
-    quarter = turns.astype(jnp.int32)
-    swap = (quarter & 1) == 1
-    sin_x = jnp.where(swap, cos_r, sin_r)
-    cos_x = jnp.where(swap, sin_r, cos_r)
-    sin_x = jnp.where((quarter & 2) == 2, -sin_x, sin_x)
-    cos_x = jnp.where(((quarter + 1) & 2) == 2, -cos_x, cos_x)
-    return sin_x, cos_x
-
-
-def phases_body(classes, scalars, detail, phase_re, phase_im, lens_re, lens_im, kinds_of):
+    y = x * 0.25
+    z = y * y
+    s = y + y * z * (-1 / 6 + z * (1 / 120 + z * (-1 / 5040 + z * (1 / 362880 + z * (-1 / 39916800)))))
+    c = 1.0 + z * (-1 / 2 + z * (1 / 24 + z * (-1 / 720 + z * (1 / 40320 + z * (-1 / 3628800 + z * (1 / 479001600))))))
+    s2 = s * c
+    s2 = s2 + s2
+    c2 = 1.0 - 2.0 * (s * s)
+    s4 = s2 * c2
+    return s4 + s4, 1.0 - 2.0 * (s2 * s2)
+
+
+def opening_body(angular, fields, basis_hbm, basis_t_hbm, classes_hbm, slow_hbm, detail_hbm,
+                 basis, basis_t, phase_re, phase_im, lens_re, lens_im, receiver, out,
+                 classes, class_slow, detail, kinds_of, wide, tall, spectrum, start, sems):
+    pairs = (
+        (fields.at[0, 0, 0], start),
+        (basis_hbm, basis),
+        (basis_t_hbm, basis_t),
+        (classes_hbm, classes),
+        (slow_hbm, class_slow),
+        (detail_hbm, detail),
+        (fields.at[0, 1, 0], receiver),
+    )
+    copies = [pltpu.make_async_copy(a, b, sems.at[k]) for k, (a, b) in enumerate(pairs)]
+    for copy in copies:
+        copy.start()
+    for copy in copies[:3]:
+        copy.wait()
+    spectrum[...] = to_spectrum(start[...].reshape(tall.shape), basis, basis_t, wide)
     lateral = detail.shape[0]
     blocks = lateral // BLOCK
     half = lateral // 2
@@ -59,17 +71,19 @@
         return kappa * kappa, weight
 
     lane_sq, lane_weight = axis_terms((1, lateral), 1, 0)
+    for copy in copies[3:5]:
+        copy.wait()
     for i in range(blocks):
         kinds_of[i : i + 1, :] = classes[i]
     kinds = kinds_of[...]
     slow = jnp.zeros(kinds.shape, F32)
-    count = scalars.shape[1] - 1
-    for kind in range(count):
-        slow = jnp.where(kinds == kind, scalars[0:1, kind : kind + 1], slow)
-    w = scalars[0:1, count : count + 1]
+    for kind in range(class_slow.shape[1]):
+        slow = jnp.where(kinds == kind, class_slow[0:1, kind : kind + 1], slow)
+    w = angular[0]
     spread = jnp.zeros((blocks, lateral), F32)
     for j in range(blocks):
         spread = jnp.where(lane_block == j, slow[:, j : j + 1], spread)
+    copies[5].wait()
     total = jnp.zeros((8, lateral), F32)
     for i in range(blocks):
         cells = spread[i : i + 1, :] * detail[i * BLOCK : (i + 1) * BLOCK, :]
@@ -110,14 +124,27 @@
 
     lax.fori_loop(0, half // rows, spectral, 0, unroll=2)
     phase_re[half : half + 8, :], phase_im[half : half + 8, :] = phases(half, 8)
+    from_spectrum(
+        spectrum[...], basis, basis_t, phase_re, phase_im, lens_re, lens_im, wide, tall, put(out)
+    )
+    copies[6].wait()
 
 
 def step_core(start, basis, basis_t, phase_re, phase_im, lens_re, lens_im, wide, tall, write):
+    spectrum = to_spectrum(start, basis, basis_t, wide)
+    from_spectrum(spectrum, basis, basis_t, phase_re, phase_im, lens_re, lens_im, wide, tall, write)
+
+
+def to_spectrum(start, basis, basis_t, wide):
     n = basis.shape[0]
     first = jnp.dot(start, basis[...], preferred_element_type=F32).astype(BF16)
     wide[:, :n] = first[:n]
     wide[:, n:] = first[n:]
-    spectrum = jnp.dot(basis_t[...], wide[...], preferred_element_type=F32)
+    return jnp.dot(basis_t[...], wide[...], preferred_element_type=F32)
+
+
+def from_spectrum(spectrum, basis, basis_t, phase_re, phase_im, lens_re, lens_im, wide, tall, write):
+    n = basis.shape[0]
     spec_re, spec_im = spectrum[:, :n], spectrum[:, n:]
     wide[:, :n] = (spec_re * phase_re[...] - spec_im * phase_im[...]).astype(BF16)
     wide[:, n:] = (spec_re * phase_im[...] + spec_im * phase_re[...]).astype(BF16)
@@ -157,12 +184,6 @@
 TABLES = 6
 
 
-def first_body(start, *refs):
-    tables, (out, wide, tall) = refs[:TABLES], refs[TABLES:]
-    n = start.shape[-1]
-    step_core(start[0, 0, 0].reshape(2 * n, n), *tables, wide, tall, put(out))
-
-
 def later_body(tick, arrived, surface, *refs):
     tables, (out, wide, tall) = refs[:TABLES], refs[TABLES:]
     step_core(entering(arrived, surface, tick, 0, tall), *tables, wide, tall, put(out))
@@ -186,7 +207,7 @@
 def first_image_body(start, source, *refs):
     tables, (out, image, illum, wide, tall) = refs[:TABLES], refs[TABLES:]
     n = start.shape[-1]
-    step_core(start[0, 1, 0].reshape(2 * n, n), *tables, wide, tall, put(out))
+    step_core(start[...].reshape(2 * n, n), *tables, wide, tall, put(out))
     image[...], illum[...] = add_terms(source, out, 0.0, 0.0)
 
 
@@ -302,36 +323,35 @@
     rows = n // peers
     lit = rows * n // 128
     basis, basis_t = (jnp.asarray(table) for table in transform_tables(n))
-    scalars = jnp.concatenate([class_slowness, angular_freq])[None]
-    kinds = velocity_class.transpose(1, 0, 2)
-    scratch = [pltpu.VMEM((kinds.shape[0], kinds.shape[2]), jnp.int32)]
-    phases = call(phases_body, [vmem] * 3, [cells] * 4, scratch)(kinds, scalars, slowness_detail[0])
-    tables = (basis, basis_t, *phases)
-    source = call(first_body, [vmem] * (1 + TABLES), field, work)(fields_top, *tables)
+    small = (velocity_class.transpose(1, 0, 2), class_slowness[None], slowness_detail[0])
+    whole = (fields_top, basis, basis_t, *small)
+    table = jax.ShapeDtypeStruct((n, n), BF16)
+    scratch = [pltpu.VMEM(a.shape, a.dtype) for a in small]
+    scratch += [pltpu.VMEM((small[0].shape[0], small[0].shape[2]), jnp.int32)] + work
+    scratch += [pltpu.VMEM((n, 2 * n), F32), pltpu.VMEM((2, n, n), BF16), pltpu.SemaphoreType.DMA((7,))]
+    *tables, receiver_top, source = call(
+        opening_body,
+        [pl.BlockSpec(memory_space=pltpu.SMEM)] + [pl.BlockSpec(memory_space=pltpu.HBM)] * len(whole),
+        [table] * 2 + [cells] * 4 + [field] * 2,
+        scratch,
+    )(angular_freq, *(pltpu.with_memory_space_constraint(a, pltpu.HBM) for a in whole))
     sent_source = passed_along(source, "depth", 1)
     receiver, image, illum = call(
         first_image_body, [vmem] * (2 + TABLES), [field, cells, cells], work
-    )(fields_top, source, *tables)
+    )(receiver_top, source, *tables)
     rising = passed_along(up_state[0, 0], "depth", -1)
     for tick in range(1, TICKS):
         sent_receiver = passed_along(receiver, "depth", 1)
-        source = call(
-            partial(later_body, tick), [vmem] * (2 + TABLES), field, work
-        )(sent_source, surface, *tables)
+        source = call(partial(later_body, tick), [vmem] * (2 + TABLES), field, work)(sent_source, surface, *tables)
         args = (sent_receiver, surface, source, image, illum, *tables)
         specs = [vmem] * (5 + TABLES)
         if tick + 1 < TICKS:
             sent_source = passed_along(source, "depth", 1)
-            receiver, image, illum = call(
-                partial(later_image_body, tick), specs, [field, cells, cells], work
-            )(*args)
+            receiver, image, illum = call(partial(later_image_body, tick), specs, [field, cells, cells], work)(*args)
         else:
             parcel = jax.ShapeDtypeStruct((peers, 2 * lit + 16, 128), BF16)
             parcel = call(
-                partial(last_image_body, tick),
-                [vmem] + specs,
-                parcel,
-                work + [pltpu.VMEM((2, n, n), BF16)],
+                partial(last_image_body, tick), [vmem] + specs, parcel, work + [pltpu.VMEM((2, n, n), BF16)]
             )(rising, *args)
     balanced = jax.ShapeDtypeStruct((peers, lit + 8, 128), BF16)
     balanced = call(balance_body, [vmem], balanced, [])(exchanged(parcel))

time: 79.6 us -> 77.5 us (0.974)
  local copies, waits for them, and re-layouts: 1.79 us -> 0.01 us
    unnamed x14 -> x4, local copies, waits for them, and re-layouts: 1.79 us -> 0.01 us
    pallas_call x2 -> x1, Pallas kernels: 4.45 us -> 5.16 us  [per_device(): call(opening_body, [pl.BlockSpec(memory_space=pltpu.SMEM)] + [pl.BlockSpe...]
where the time goes in v1:
time: 77.5 us; the launch traced here: 77.2 us
  blocking collectives  33.5 us (43%)
  Pallas kernels  19.5 us (25%)
  starting transfers between devices  15.9 us (21%)
  waiting for transfers between devices  6.87 us (9%)
  between operations  1.4 us (2%)
    all_to_all x2, blocking collectives, exchanged(): lax.all_to_all(parcel, 'freq', split_axis=0, concat_axis=0, tiled=True)  33.5 us
    ppermute x5, starting transfers between devices, passed_along(): return lax.ppermute(block, axis, route)  15.9 us
    ppermute x5, waiting for transfers between devices, passed_along(): return lax.ppermute(block, axis, route)  6.87 us
    pallas_call x1, Pallas kernels, per_device(): call(opening_body, [pl.BlockSpec(memory_space=pltpu.SMEM)] + [pl.BlockSpe...  5.16 us
    pallas_call x2, Pallas kernels, per_device(): call(partial(later_body, tick), [vmem] * (2 + TABLES), field, work)  4 us
    pallas_call x1, Pallas kernels, per_device(): call(upward_body, [vmem] * (3 + TABLES), [jax.ShapeDtypeStruct((rows, n),...  2.98 us
    pallas_call x1, Pallas kernels, per_device(): call(partial(last_image_body, tick), [vmem] + specs, parcel, work + [pltp...  2.66 us
    pallas_call x1, Pallas kernels, per_device(): call(partial(later_image_body, tick), specs, [field, cells, cells], work)  2.25 us
  transfers between devices with their start and end apart: 5, of which 3 were waited for; matrix products, arithmetic and copies ran while one was open for 0% of the time, Pallas kernels for 11%

profile of v1, /device:TPU:96, one launch (start us, length us, event | category | flops | bytes accessed | tf_op | source)
XLA Modules:
  0.0 77.2 jit_solution(4289381931150372474)
XLA Ops:
  1.3 5.2 %shard_map.104 = (bf16[384,384]{1,0:T(8,128)(2,1)S(1)}, bf16[384,384]{1,0:T(8,128)(2,1)S(1)}, f32[384,384]{1,0:T(8,128)S(1)}, f32[384,384]{1,0:T(8,128)S(1)}, f3...) custom-call(f32[1]{0:T(128)S(6)} %copy.11.angular, ...), custom_call_target="tpu_custom_call" | custom-call | flops 905969664 | bytes 1179648 | tf_op jit(solution)/shard_map/pallas_call | solution.py:332
  6.4 0.0 copy-start.1
  6.5 0.0 copy-start
  6.5 2.2 %collective-permute-start.2 = (bf16[2,384,384]{2,1,0:T(8,128)(2,1)S(1)}, bf16[2,384,384]{2,1,0:T(8,128)(2,1)S(1)}, u32[]{:S(2)}, u32[]{:S(2)}) collective-permute-start(bf16[2,384,384]{2,1,0:T(8,128)(2,1)S(1)} %get-tuple-element.19.source), channel_id=1, source_target_pairs={{0,16},{16,32},{32,48},{48,64},{64,80},{80,96},{96,112},{112,128},... | collective-permute-start | bytes 1769480 | tf_op jit(solution)/shard_map/ppermute | solution.py:294
  8.7 2.2 %shard_map.105 = (bf16[2,384,384]{2,1,0:T(8,128)(2,1)S(1)}, f32[384,384]{1,0:T(8,128)S(1)}, f32[384,384]{1,0:T(8,128)S(1)}) custom-call(bf16[2,384,384]{2,1,0:T(8,128)(2,1)S(1)} %get-tuple-element.18.start, bf16[2,384,384]{2,1,0:T(8,128)(2,1)S(1)} %get-tuple-element.19.source, bf16[384,384]{1,0:T(8,128)(2,1)S(1)} %get-tuple-element.20.refs_0_, ...), custom_call_target="tpu_custom_call" | custom-call | flops 905969664 | bytes 1179648 | tf_op jit(solution)/shard_map/pallas_call | solution.py:339
  10.8 5.1 %collective-permute-start.1 = (bf16[2,384,384]{2,1,0:T(8,128)(2,1)S(1)}, bf16[2,384,384]{2,1,0:T(8,128)(2,1)S(1)}, u32[]{:S(2)}, u32[]{:S(2)}) collective-permute-start(bf16[2,384,384]{2,1,0:T(8,128)(2,1)S(1)} %get-tuple-element.26), channel_id=1, source_target_pairs={{0,16},{16,32},{32,48},{48,64},{64,80},{80,96},{96,112},{112,128},... | collective-permute-start | bytes 1769480 | tf_op jit(solution)/shard_map/ppermute | solution.py:294
  16.0 0.0 copy-done.1
  16.0 1.9 %collective-permute-start = (bf16[2,384,384]{2,1,0:T(8,128)(2,1)S(1)}, bf16[2,384,384]{2,1,0:T(8,128)(2,1)S(1)}, u32[]{:S(2)}, u32[]{:S(2)}) collective-permute-start(bf16[2,384,384]{2,1,0:T(8,128)(2,1)S(1)} %bitcast.7), channel_id=1, source_target_pairs={{16,0},{32,16},{48,32},{64,48},{80,64},{96,80},{112,96},{128,112},... | collective-permute-start | bytes 1769480 | tf_op jit(solution)/shard_map/ppermute | solution.py:294
  17.9 0.0 collective-permute-done.2.arrived
  17.9 0.0 copy-done
  17.9 2.0 %shard_map.106.source = bf16[2,384,384]{2,1,0:T(8,128)(2,1)S(1)} custom-call(bf16[2,384,384]{2,1,0:T(8,128)(2,1)S(1)} %collective-permute-done.2.arrived, bf16[2,2,1,2,384,384]{5,4,3,2,1,0:T(8,128)(2,1)S(1)} %copy-done, bf16[384,384]{1,0:T(8,128)(2,1)S(1)} %get-tuple-element.20.refs_0_, bf16[384,384]{1,0:T(8,128)(2,1)S(1)} %get-tuple-element.21.refs_1_, ...), custom_call_target="tpu_custom_call" | custom-call | flops 905969664 | bytes 1179648 | tf_op jit(solution)/shard_map/pallas_call | solution.py:345
  19.9 2.7 %collective-permute-start.4 = (bf16[2,384,384]{2,1,0:T(8,128)(2,1)S(1)}, bf16[2,384,384]{2,1,0:T(8,128)(2,1)S(1)}, u32[]{:S(2)}, u32[]{:S(2)}) collective-permute-start(bf16[2,384,384]{2,1,0:T(8,128)(2,1)S(1)} %shard_map.106.source), channel_id=1, source_target_pairs={{0,16},{16,32},{32,48},{48,64},{64,80},{80,96},{96,112},{112,128},... | collective-permute-start | bytes 1769480 | tf_op jit(solution)/shard_map/ppermute | solution.py:294
  22.6 1.6 %collective-permute-done.1.arrived = bf16[2,384,384]{2,1,0:T(8,128)(2,1)S(1)} collective-permute-done((bf16[2,384,384]{2,1,0:T(8,128)(2,1)S(1)}, bf16[2,384,384]{2,1,0:T(8,128)(2,1)S(1)}, u32[]{:S(2)}, u32[]{:S(2)}) %collective-permute-start.1) | collective-permute-done | bytes 589856 | tf_op jit(solution)/shard_map/ppermute | solution.py:294
  24.2 2.2 %shard_map.107 = (bf16[2,384,384]{2,1,0:T(8,128)(2,1)S(1)}, f32[384,384]{1,0:T(8,128)S(1)}, f32[384,384]{1,0:T(8,128)S(1)}) custom-call(bf16[2,384,384]{2,1,0:T(8,128)(2,1)S(1)} %collective-permute-done.1.arrived, bf16[2,2,1,2,384,384]{5,4,3,2,1,0:T(8,128)(2,1)S(1)} %copy-done, bf16[2,384,384]{2,1,0:T(8,128)(2,1)S(1)} %shard_map.106.source, ...), custom_call_target="tpu_custom_call" | custom-call | flops 905969664 | bytes 1179648 | tf_op jit(solution)/shard_map/pallas_call | solution.py:350
  26.5 4.0 %collective-permute-start.3 = (bf16[2,384,384]{2,1,0:T(8,128)(2,1)S(1)}, bf16[2,384,384]{2,1,0:T(8,128)(2,1)S(1)}, u32[]{:S(2)}, u32[]{:S(2)}) collective-permute-start(bf16[2,384,384]{2,1,0:T(8,128)(2,1)S(1)} %get-tuple-element.29), channel_id=1, source_target_pairs={{0,16},{16,32},{32,48},{48,64},{64,80},{80,96},{96,112},{112,128},... | collective-permute-start | bytes 1769480 | tf_op jit(solution)/shard_map/ppermute | solution.py:294
  30.5 0.6 collective-permute-done.4.arrived
  31.1 2.0 %shard_map.108.source = bf16[2,384,384]{2,1,0:T(8,128)(2,1)S(1)} custom-call(bf16[2,384,384]{2,1,0:T(8,128)(2,1)S(1)} %collective-permute-done.4.arrived, bf16[2,2,1,2,384,384]{5,4,3,2,1,0:T(8,128)(2,1)S(1)} %copy-done, bf16[384,384]{1,0:T(8,128)(2,1)S(1)} %get-tuple-element.20.refs_0_, bf16[384,384]{1,0:T(8,128)(2,1)S(1)} %get-tuple-element.21.refs_1_, ...), custom_call_target="tpu_custom_call" | custom-call | flops 905969664 | bytes 1179648 | tf_op jit(solution)/shard_map/pallas_call | solution.py:345
  33.1 0.0 collective-permute-done.rising
  33.2 4.6 %collective-permute-done.3.arrived = bf16[2,384,384]{2,1,0:T(8,128)(2,1)S(1)} collective-permute-done((bf16[2,384,384]{2,1,0:T(8,128)(2,1)S(1)}, bf16[2,384,384]{2,1,0:T(8,128)(2,1)S(1)}, u32[]{:S(2)}, u32[]{:S(2)}) %collective-permute-start.3) | collective-permute-done | bytes 589856 | tf_op jit(solution)/shard_map/ppermute | solution.py:294
  37.7 2.7 %shard_map.109 = bf16[16,160,128]{2,1,0:T(8,128)(2,1)S(1)} custom-call(bf16[2,384,384]{2,1,0:T(8,128)(2,1)S(1)} %collective-permute-done.rising, bf16[2,384,384]{2,1,0:T(8,128)(2,1)S(1)} %collective-permute-done.3.arrived, bf16[2,2,1,2,384,384]{5,4,3,2,1,0:T(8,128)(2,1)S(1)} %copy-done, bf16[2,384,384]{2,1,0:T(8,128)(2,1)S(1)} %shard_map.108.source, ...), custom_call_target="tpu_custom_call" | custom-call | flops 905969664 | bytes 1179648 | tf_op jit(solution)/shard_map/pallas_call | solution.py:353
  40.4 20.1 %all_to_all.10.parcel = bf16[16,160,128]{2,1,0:T(8,128)(2,1)S(1)} all-to-all(bf16[16,160,128]{2,1,0:T(8,128)(2,1)S(1)} %shard_map.109), channel_id=1, replica_groups=mesh['depth'=16,'freq'=16] {'freq'}, dimensions={0} | all-to-all | bytes 1310720 | tf_op jit(solution)/shard_map/all_to_all | solution.py:298
  60.5 0.3 shard_map.110
  60.8 13.5 %all_to_all.11.parcel = bf16[16,80,128]{2,1,0:T(8,128)(2,1)S(1)} all-to-all(bf16[16,80,128]{2,1,0:T(8,128)(2,1)S(1)} %shard_map.110), channel_id=1, replica_groups=mesh['depth'=16,'freq'=16] {'freq'}, dimensions={0} | all-to-all | bytes 655360 | tf_op jit(solution)/shard_map/all_to_all | solution.py:298
  74.2 3.0 %shard_map.111 = (bf16[24,384]{1,0:T(8,128)(2,1)}, bf16[2,384,384]{2,1,0:T(8,128)(2,1)}) custom-call(bf16[16,80,128]{2,1,0:T(8,128)(2,1)S(1)} %all_to_all.11.parcel, bf16[2,384,384]{2,1,0:T(8,128)(2,1)S(1)} %collective-permute-done.rising, bf16[2,384,384]{2,1,0:T(8,128)(2,1)S(1)} %shard_map.108.source, bf16[384,384]{1,0:T(8,128)(2,1)S(1)} %get-tuple-element.20.refs_0_, ...), custom_call_target="tpu_custom_call" | custom-call | flops 905969664 | bytes 1179648 | tf_op jit(solution)/shard_map/pallas_call | solution.py:358
Async XLA Ops:
  6.4 9.5 %copy-start.1 = (bf16[1,1,2,384,384]{4,3,2,1,0:T(8,128)(2,1)S(1)}, bf16[1,1,2,384,384]{4,3,2,1,0:T(8,128)(2,1)}, u32[]{:S(2)}) copy-start(bf16[1,1,2,384,384]{4,3,2,1,0:T(8,128)(2,1)} %param.11) | copy-start | bytes 1769476
  6.5 11.5 %copy-start = (bf16[2,2,1,2,384,384]{5,4,3,2,1,0:T(8,128)(2,1)S(1)}, bf16[2,2,1,2,384,384]{5,4,3,2,1,0:T(8,128)(2,1)}, u32[]{:S(2)}) copy-start(bf16[2,2,1,2,384,384]{5,4,3,2,1,0:T(8,128)(2,1)} %surface.7) | copy-start | bytes 7077892
  6.5 11.5 %collective-permute-start.2 = (bf16[2,384,384]{2,1,0:T(8,128)(2,1)S(1)}, bf16[2,384,384]{2,1,0:T(8,128)(2,1)S(1)}, u32[]{:S(2)}, u32[]{:S(2)}) collective-permute-start(bf16[2,384,384]{2,1,0:T(8,128)(2,1)S(1)} %get-tuple-element.19.source), channel_id=1, source_target_pairs={{0,16},{16,32},{32,48},{48,64},{64,80},{80,96},{96,112},{112,128},... | collective-permute-start | bytes 1769480 | tf_op jit(solution)/shard_map/ppermute | solution.py:294
  10.8 13.4 %collective-permute-start.1 = (bf16[2,384,384]{2,1,0:T(8,128)(2,1)S(1)}, bf16[2,384,384]{2,1,0:T(8,128)(2,1)S(1)}, u32[]{:S(2)}, u32[]{:S(2)}) collective-permute-start(bf16[2,384,384]{2,1,0:T(8,128)(2,1)S(1)} %get-tuple-element.26), channel_id=1, source_target_pairs={{0,16},{16,32},{32,48},{48,64},{64,80},{80,96},{96,112},{112,128},... | collective-permute-start | bytes 1769480 | tf_op jit(solution)/shard_map/ppermute | solution.py:294
  16.0 17.2 %collective-permute-start = (bf16[2,384,384]{2,1,0:T(8,128)(2,1)S(1)}, bf16[2,384,384]{2,1,0:T(8,128)(2,1)S(1)}, u32[]{:S(2)}, u32[]{:S(2)}) collective-permute-start(bf16[2,384,384]{2,1,0:T(8,128)(2,1)S(1)} %bitcast.7), channel_id=1, source_target_pairs={{16,0},{32,16},{48,32},{64,48},{80,64},{96,80},{112,96},{128,112},... | collective-permute-start | bytes 1769480 | tf_op jit(solution)/shard_map/ppermute | solution.py:294
  19.9 11.2 %collective-permute-start.4 = (bf16[2,384,384]{2,1,0:T(8,128)(2,1)S(1)}, bf16[2,384,384]{2,1,0:T(8,128)(2,1)S(1)}, u32[]{:S(2)}, u32[]{:S(2)}) collective-permute-start(bf16[2,384,384]{2,1,0:T(8,128)(2,1)S(1)} %shard_map.106.source), channel_id=1, source_target_pairs={{0,16},{16,32},{32,48},{48,64},{64,80},{80,96},{96,112},{112,128},... | collective-permute-start | bytes 1769480 | tf_op jit(solution)/shard_map/ppermute | solution.py:294
  26.5 11.2 %collective-permute-start.3 = (bf16[2,384,384]{2,1,0:T(8,128)(2,1)S(1)}, bf16[2,384,384]{2,1,0:T(8,128)(2,1)S(1)}, u32[]{:S(2)}, u32[]{:S(2)}) collective-permute-start(bf16[2,384,384]{2,1,0:T(8,128)(2,1)S(1)} %get-tuple-element.29), channel_id=1, source_target_pairs={{0,16},{16,32},{32,48},{48,64},{64,80},{80,96},{96,112},{112,128},... | collective-permute-start | bytes 1769480 | tf_op jit(solution)/shard_map/ppermute | solution.py:294

commit v2 on v1

--- a/solution.py
+++ b/solution.py
@@ -104,15 +104,6 @@
 
     rows = 32
 
-    def lens(index, carry):
-        here = pl.ds(pl.multiple_of(index * rows, rows), rows)
-        lens_sin, lens_cos = sincos(scale * (lens_re[here, :] - mean))
-        lens_re[here, :] = lens_cos
-        lens_im[here, :] = lens_sin
-        return carry
-
-    lax.fori_loop(0, lateral // rows, lens, 0, unroll=2)
-
     def spectral(index, carry):
         start = pl.multiple_of(index * rows, rows)
         real, imag = phases(start, rows)
@@ -124,6 +115,11 @@
 
     lax.fori_loop(0, half // rows, spectral, 0, unroll=2)
     phase_re[half : half + 8, :], phase_im[half : half + 8, :] = phases(half, 8)
+    for first in range(0, lateral, rows):
+        here = slice(first, first + rows)
+        lens_sin, lens_cos = sincos(scale * (lens_re[here, :] - mean))
+        lens_re[here, :] = lens_cos
+        lens_im[here, :] = lens_sin
     from_spectrum(
         spectrum[...], basis, basis_t, phase_re, phase_im, lens_re, lens_im, wide, tall, put(out)
     )
@@ -217,8 +213,9 @@
     image[...], illum[...] = add_terms(source, out, image_in[...], illum_in[...])
 
 
-def last_image_body(tick, rising, arrived, surface, source, image_in, illum_in, *refs):
-    tables, (parcel, wide, tall, out) = refs[:TABLES], refs[TABLES:]
+def last_source_body(tick, arrived, surface, illum_in, *refs):
+    tables, (out, parcel, wide, tall) = refs[:TABLES], refs[TABLES:]
+    step_core(entering(arrived, surface, tick, 0, tall), *tables, wide, tall, put(out))
     peers = parcel.shape[0]
     n = illum_in.shape[0]
     rows = n // peers
@@ -226,7 +223,7 @@
     total = jnp.zeros((rows, n), F32)
     for peer in range(peers):
         here = slice(peer * rows, (peer + 1) * rows)
-        s_re, s_im = source[0, here, :].astype(F32), source[1, here, :].astype(F32)
+        s_re, s_im = out[0, here, :].astype(F32), out[1, here, :].astype(F32)
         illum = illum_in[here, :] + (s_re * s_re + s_im * s_im)
         total = total + illum
         small = illum.astype(BF16)
@@ -236,6 +233,14 @@
     extra = pieces(jnp.sum(total), 16)
     for peer in range(peers):
         parcel[peer, 2 * lit : 2 * lit + 16, :] = extra
+        parcel[peer, 0:lit, :] = jnp.zeros((lit, 128), BF16)
+
+
+def last_image_body(tick, begun, rising, arrived, surface, source, image_in, *refs):
+    tables, (parcel, wide, tall, out) = refs[:TABLES], refs[TABLES:]
+    peers = parcel.shape[0]
+    n = image_in.shape[0]
+    rows = n // peers
     step_core(entering(arrived, surface, tick, 1, tall), *tables, wide, tall, put(out))
     for peer in range(peers):
         here = slice(peer * rows, (peer + 1) * rows)
@@ -309,7 +314,7 @@
     work = [pltpu.VMEM((n, 2 * n), BF16), pltpu.VMEM((2 * n, n), BF16)]
     cost = pl.CostEstimate(flops=2 * 4 * 2 * n**3, transcendentals=0, bytes_accessed=8 * n * n)
 
-    def call(body, in_specs, out_shape, scratch):
+    def call(body, in_specs, out_shape, scratch, aliases={}):
         return pl.pallas_call(
             body,
             in_specs=in_specs,
@@ -318,6 +323,7 @@
             scratch_shapes=scratch,
             cost_estimate=cost,
             compiler_params=pltpu.CompilerParams(vmem_limit_bytes=14 << 20),
+            input_output_aliases=aliases,
         )
 
     rows = n // peers
@@ -340,19 +346,33 @@
         first_image_body, [vmem] * (2 + TABLES), [field, cells, cells], work
     )(receiver_top, source, *tables)
     rising = passed_along(up_state[0, 0], "depth", -1)
+    parcel_shape = jax.ShapeDtypeStruct((peers, 2 * lit + 16, 128), BF16)
     for tick in range(1, TICKS):
         sent_receiver = passed_along(receiver, "depth", 1)
-        source = call(partial(later_body, tick), [vmem] * (2 + TABLES), field, work)(sent_source, surface, *tables)
-        args = (sent_receiver, surface, source, image, illum, *tables)
-        specs = [vmem] * (5 + TABLES)
-        if tick + 1 < TICKS:
+        last = tick + 1 == TICKS
+        args = (sent_source, surface, illum, *tables) if last else (sent_source, surface, *tables)
+        made = call(
+            partial(last_source_body if last else later_body, tick),
+            [vmem] * len(args),
+            [field, parcel_shape] if last else [field],
+            work,
+        )(*args)
+        source = made[0]
+        args = (sent_receiver, surface, source, image)
+        if not last:
             sent_source = passed_along(source, "depth", 1)
-            receiver, image, illum = call(partial(later_image_body, tick), specs, [field, cells, cells], work)(*args)
-        else:
-            parcel = jax.ShapeDtypeStruct((peers, 2 * lit + 16, 128), BF16)
-            parcel = call(
-                partial(last_image_body, tick), [vmem] + specs, parcel, work + [pltpu.VMEM((2, n, n), BF16)]
-            )(rising, *args)
+            args = (*args, illum, *tables)
+            receiver, image, illum = call(
+                partial(later_image_body, tick), [vmem] * len(args), [field, cells, cells], work
+            )(*args)
+    args = (made[1], rising, *args, *tables)
+    parcel = call(
+        partial(last_image_body, TICKS - 1),
+        [vmem] * len(args),
+        parcel_shape,
+        work + [pltpu.VMEM((2, n, n), BF16)],
+        {0: 0},
+    )(*args)
     balanced = jax.ShapeDtypeStruct((peers, lit + 8, 128), BF16)
     balanced = call(balance_body, [vmem], balanced, [])(exchanged(parcel))
     part, risen = call(

time: 77.5 us -> 77 us (level)
  no operation moved by 1% of the time
where the time goes in v2:
time: 77 us; the launch traced here: 76.7 us
  blocking collectives  33.5 us (44%)
  Pallas kernels  19.3 us (25%)
  starting transfers between devices  15.9 us (21%)
  waiting for transfers between devices  6.54 us (8%)
  between operations  1.4 us (2%)
    all_to_all x2, blocking collectives, exchanged(): lax.all_to_all(parcel, 'freq', split_axis=0, concat_axis=0, tiled=True)  33.5 us
    ppermute x5, starting transfers between devices, passed_along(): return lax.ppermute(block, axis, route)  15.9 us
    ppermute x5, waiting for transfers between devices, passed_along(): return lax.ppermute(block, axis, route)  6.54 us
    pallas_call x1, Pallas kernels, per_device(): call(opening_body, [pl.BlockSpec(memory_space=pltpu.SMEM)] + [pl.BlockSpe...  4.98 us
    pallas_call x2, Pallas kernels, per_device(): call(partial(last_source_body if last else later_body, tick), [vmem] * le...  4.31 us
    pallas_call x1, Pallas kernels, per_device(): call(upward_body, [vmem] * (3 + TABLES), [jax.ShapeDtypeStruct((rows, n),...  2.98 us
    pallas_call x1, Pallas kernels, per_device(): call(partial(last_image_body, TICKS - 1), [vmem] * len(args), parcel_shap...  2.37 us
    pallas_call x1, Pallas kernels, per_device(): call(partial(later_image_body, tick), [vmem] * len(args), [field, cells,...  2.24 us
  transfers between devices with their start and end apart: 5, of which 3 were waited for; matrix products, arithmetic and copies ran while one was open for 0% of the time, Pallas kernels for 11%

profile of v2, /device:TPU:96, one launch (start us, length us, event | category | flops | bytes accessed | tf_op | source)
XLA Modules:
  0.0 76.7 jit_solution(13269010767699015788)
XLA Ops:
  1.3 5.0 %shard_map.104 = (bf16[384,384]{1,0:T(8,128)(2,1)S(1)}, bf16[384,384]{1,0:T(8,128)(2,1)S(1)}, f32[384,384]{1,0:T(8,128)S(1)}, f32[384,384]{1,0:T(8,128)S(1)}, f3...) custom-call(f32[1]{0:T(128)S(6)} %copy.13.angular, ...), custom_call_target="tpu_custom_call" | custom-call | flops 905969664 | bytes 1179648 | tf_op jit(solution)/shard_map/pallas_call | solution.py:338
  6.3 0.0 copy-start.1
  6.3 0.0 copy-start
  6.3 2.2 %collective-permute-start = (bf16[2,384,384]{2,1,0:T(8,128)(2,1)S(1)}, bf16[2,384,384]{2,1,0:T(8,128)(2,1)S(1)}, u32[]{:S(2)}, u32[]{:S(2)}) collective-permute-start(bf16[2,384,384]{2,1,0:T(8,128)(2,1)S(1)} %get-tuple-element.20.source), channel_id=1, source_target_pairs={{0,16},{16,32},{32,48},{48,64},{64,80},{80,96},{96,112},{112,128},... | collective-permute-start | bytes 1769480 | tf_op jit(solution)/shard_map/ppermute | solution.py:299
  8.5 2.2 %shard_map.106 = (bf16[2,384,384]{2,1,0:T(8,128)(2,1)S(1)}, f32[384,384]{1,0:T(8,128)S(1)}, f32[384,384]{1,0:T(8,128)S(1)}) custom-call(bf16[2,384,384]{2,1,0:T(8,128)(2,1)S(1)} %get-tuple-element.27.start, bf16[2,384,384]{2,1,0:T(8,128)(2,1)S(1)} %get-tuple-element.20.source, bf16[384,384]{1,0:T(8,128)(2,1)S(1)} %get-tuple-element.21.refs_0_, ...), custom_call_target="tpu_custom_call" | custom-call | flops 905969664 | bytes 1179648 | tf_op jit(solution)/shard_map/pallas_call | solution.py:345
  10.6 5.1 %collective-permute-start.2 = (bf16[2,384,384]{2,1,0:T(8,128)(2,1)S(1)}, bf16[2,384,384]{2,1,0:T(8,128)(2,1)S(1)}, u32[]{:S(2)}, u32[]{:S(2)}) collective-permute-start(bf16[2,384,384]{2,1,0:T(8,128)(2,1)S(1)} %get-tuple-element.28), channel_id=1, source_target_pairs={{0,16},{16,32},{32,48},{48,64},{64,80},{80,96},{96,112},{112,128},... | collective-permute-start | bytes 1769480 | tf_op jit(solution)/shard_map/ppermute | solution.py:299
  15.8 0.0 copy-done.1
  15.8 1.9 %collective-permute-start.3 = (bf16[2,384,384]{2,1,0:T(8,128)(2,1)S(1)}, bf16[2,384,384]{2,1,0:T(8,128)(2,1)S(1)}, u32[]{:S(2)}, u32[]{:S(2)}) collective-permute-start(bf16[2,384,384]{2,1,0:T(8,128)(2,1)S(1)} %bitcast.7), channel_id=1, source_target_pairs={{16,0},{32,16},{48,32},{64,48},{80,64},{96,80},{112,96},{128,112},... | collective-permute-start | bytes 1769480 | tf_op jit(solution)/shard_map/ppermute | solution.py:299
  17.7 0.0 collective-permute-done.arrived
  17.8 0.0 copy-done
  17.8 2.0 %shard_map.105.source = bf16[2,384,384]{2,1,0:T(8,128)(2,1)S(1)} custom-call(bf16[2,384,384]{2,1,0:T(8,128)(2,1)S(1)} %collective-permute-done.arrived, bf16[2,2,1,2,384,384]{5,4,3,2,1,0:T(8,128)(2,1)S(1)} %copy-done, bf16[384,384]{1,0:T(8,128)(2,1)S(1)} %get-tuple-element.21.refs_0_, bf16[384,384]{1,0:T(8,128)(2,1)S(1)} %get-tuple-element.22.refs_1_, ...), custom_call_target="tpu_custom_call" | custom-call | flops 905969664 | bytes 1179648 | tf_op jit(solution)/shard_map/pallas_call | solution.py:354
  19.8 2.7 %collective-permute-start.1 = (bf16[2,384,384]{2,1,0:T(8,128)(2,1)S(1)}, bf16[2,384,384]{2,1,0:T(8,128)(2,1)S(1)}, u32[]{:S(2)}, u32[]{:S(2)}) collective-permute-start(bf16[2,384,384]{2,1,0:T(8,128)(2,1)S(1)} %shard_map.105.source), channel_id=1, source_target_pairs={{0,16},{16,32},{32,48},{48,64},{64,80},{80,96},{96,112},{112,128},... | collective-permute-start | bytes 1769480 | tf_op jit(solution)/shard_map/ppermute | solution.py:299
  22.4 1.6 %collective-permute-done.2.arrived = bf16[2,384,384]{2,1,0:T(8,128)(2,1)S(1)} collective-permute-done((bf16[2,384,384]{2,1,0:T(8,128)(2,1)S(1)}, bf16[2,384,384]{2,1,0:T(8,128)(2,1)S(1)}, u32[]{:S(2)}, u32[]{:S(2)}) %collective-permute-start.2) | collective-permute-done | bytes 589856 | tf_op jit(solution)/shard_map/ppermute | solution.py:299
  24.1 2.2 %shard_map.107 = (bf16[2,384,384]{2,1,0:T(8,128)(2,1)S(1)}, f32[384,384]{1,0:T(8,128)S(1)}, f32[384,384]{1,0:T(8,128)S(1)}) custom-call(bf16[2,384,384]{2,1,0:T(8,128)(2,1)S(1)} %collective-permute-done.2.arrived, bf16[2,2,1,2,384,384]{5,4,3,2,1,0:T(8,128)(2,1)S(1)} %copy-done, bf16[2,384,384]{2,1,0:T(8,128)(2,1)S(1)} %shard_map.105.source, ...), custom_call_target="tpu_custom_call" | custom-call | flops 905969664 | bytes 1179648 | tf_op jit(solution)/shard_map/pallas_call | solution.py:365
  26.3 4.0 %collective-permute-start.4 = (bf16[2,384,384]{2,1,0:T(8,128)(2,1)S(1)}, bf16[2,384,384]{2,1,0:T(8,128)(2,1)S(1)}, u32[]{:S(2)}, u32[]{:S(2)}) collective-permute-start(bf16[2,384,384]{2,1,0:T(8,128)(2,1)S(1)} %get-tuple-element.33), channel_id=1, source_target_pairs={{0,16},{16,32},{32,48},{48,64},{64,80},{80,96},{96,112},{112,128},... | collective-permute-start | bytes 1769480 | tf_op jit(solution)/shard_map/ppermute | solution.py:299
  30.3 0.6 collective-permute-done.1.arrived
  31.0 2.3 %shard_map.108 = (bf16[2,384,384]{2,1,0:T(8,128)(2,1)S(1)}, bf16[16,160,128]{2,1,0:T(8,128)(2,1)S(1)}) custom-call(bf16[2,384,384]{2,1,0:T(8,128)(2,1)S(1)} %collective-permute-done.1.arrived, bf16[2,2,1,2,384,384]{5,4,3,2,1,0:T(8,128)(2,1)S(1)} %copy-done, f32[384,384]{1,0:T(8,128)S(1)} %get-tuple-element.31.illum_in, ...), custom_call_target="tpu_custom_call" | custom-call | flops 905969664 | bytes 1179648 | tf_op jit(solution)/shard_map/pallas_call | solution.py:354
  33.3 0.0 collective-permute-done.3.rising
  33.3 4.2 %collective-permute-done.4.arrived = bf16[2,384,384]{2,1,0:T(8,128)(2,1)S(1)} collective-permute-done((bf16[2,384,384]{2,1,0:T(8,128)(2,1)S(1)}, bf16[2,384,384]{2,1,0:T(8,128)(2,1)S(1)}, u32[]{:S(2)}, u32[]{:S(2)}) %collective-permute-start.4) | collective-permute-done | bytes 589856 | tf_op jit(solution)/shard_map/ppermute | solution.py:299
  37.5 2.4 %shard_map.109 = bf16[16,160,128]{2,1,0:T(8,128)(2,1)S(1)} custom-call(bf16[16,160,128]{2,1,0:T(8,128)(2,1)S(1)} %get-tuple-element.32.begun, bf16[2,384,384]{2,1,0:T(8,128)(2,1)S(1)} %collective-permute-done.3.rising, bf16[2,384,384]{2,1,0:T(8,128)(2,1)S(1)} %collective-permute-done.4.arrived, ...), custom_call_target="tpu_custom_call", output_to_operand_aliasing={{}: (0, {})} | custom-call | flops 905969664 | bytes 1179648 | tf_op jit(solution)/shard_map/pallas_call | solution.py:369
  39.9 20.1 %all_to_all.10.parcel = bf16[16,160,128]{2,1,0:T(8,128)(2,1)S(1)} all-to-all(bf16[16,160,128]{2,1,0:T(8,128)(2,1)S(1)} %shard_map.109), channel_id=1, replica_groups=mesh['depth'=16,'freq'=16] {'freq'}, dimensions={0} | all-to-all | bytes 1310720 | tf_op jit(solution)/shard_map/all_to_all | solution.py:303
  60.0 0.3 shard_map.110
  60.3 13.5 %all_to_all.11.parcel = bf16[16,80,128]{2,1,0:T(8,128)(2,1)S(1)} all-to-all(bf16[16,80,128]{2,1,0:T(8,128)(2,1)S(1)} %shard_map.110), channel_id=1, replica_groups=mesh['depth'=16,'freq'=16] {'freq'}, dimensions={0} | all-to-all | bytes 655360 | tf_op jit(solution)/shard_map/all_to_all | solution.py:303
  73.7 3.0 %shard_map.111 = (bf16[24,384]{1,0:T(8,128)(2,1)}, bf16[2,384,384]{2,1,0:T(8,128)(2,1)}) custom-call(bf16[16,80,128]{2,1,0:T(8,128)(2,1)S(1)} %all_to_all.11.parcel, bf16[2,384,384]{2,1,0:T(8,128)(2,1)S(1)} %collective-permute-done.3.rising, bf16[2,384,384]{2,1,0:T(8,128)(2,1)S(1)} %get-tuple-element.34.source, ...), custom_call_target="tpu_custom_call" | custom-call | flops 905969664 | bytes 1179648 | tf_op jit(solution)/shard_map/pallas_call | solution.py:378
Async XLA Ops:
  6.3 9.5 %copy-start.1 = (bf16[1,1,2,384,384]{4,3,2,1,0:T(8,128)(2,1)S(1)}, bf16[1,1,2,384,384]{4,3,2,1,0:T(8,128)(2,1)}, u32[]{:S(2)}) copy-start(bf16[1,1,2,384,384]{4,3,2,1,0:T(8,128)(2,1)} %param.11) | copy-start | bytes 1769476
  6.3 11.5 %copy-start = (bf16[2,2,1,2,384,384]{5,4,3,2,1,0:T(8,128)(2,1)S(1)}, bf16[2,2,1,2,384,384]{5,4,3,2,1,0:T(8,128)(2,1)}, u32[]{:S(2)}) copy-start(bf16[2,2,1,2,384,384]{5,4,3,2,1,0:T(8,128)(2,1)} %surface.7) | copy-start | bytes 7077892
  6.3 11.5 %collective-permute-start = (bf16[2,384,384]{2,1,0:T(8,128)(2,1)S(1)}, bf16[2,384,384]{2,1,0:T(8,128)(2,1)S(1)}, u32[]{:S(2)}, u32[]{:S(2)}) collective-permute-start(bf16[2,384,384]{2,1,0:T(8,128)(2,1)S(1)} %get-tuple-element.20.source), channel_id=1, source_target_pairs={{0,16},{16,32},{32,48},{48,64},{64,80},{80,96},{96,112},{112,128},... | collective-permute-start | bytes 1769480 | tf_op jit(solution)/shard_map/ppermute | solution.py:299
  10.6 13.4 %collective-permute-start.2 = (bf16[2,384,384]{2,1,0:T(8,128)(2,1)S(1)}, bf16[2,384,384]{2,1,0:T(8,128)(2,1)S(1)}, u32[]{:S(2)}, u32[]{:S(2)}) collective-permute-start(bf16[2,384,384]{2,1,0:T(8,128)(2,1)S(1)} %get-tuple-element.28), channel_id=1, source_target_pairs={{0,16},{16,32},{32,48},{48,64},{64,80},{80,96},{96,112},{112,128},... | collective-permute-start | bytes 1769480 | tf_op jit(solution)/shard_map/ppermute | solution.py:299
  15.8 17.5 %collective-permute-start.3 = (bf16[2,384,384]{2,1,0:T(8,128)(2,1)S(1)}, bf16[2,384,384]{2,1,0:T(8,128)(2,1)S(1)}, u32[]{:S(2)}, u32[]{:S(2)}) collective-permute-start(bf16[2,384,384]{2,1,0:T(8,128)(2,1)S(1)} %bitcast.7), channel_id=1, source_target_pairs={{16,0},{32,16},{48,32},{64,48},{80,64},{96,80},{112,96},{128,112},... | collective-permute-start | bytes 1769480 | tf_op jit(solution)/shard_map/ppermute | solution.py:299
  19.8 11.2 %collective-permute-start.1 = (bf16[2,384,384]{2,1,0:T(8,128)(2,1)S(1)}, bf16[2,384,384]{2,1,0:T(8,128)(2,1)S(1)}, u32[]{:S(2)}, u32[]{:S(2)}) collective-permute-start(bf16[2,384,384]{2,1,0:T(8,128)(2,1)S(1)} %shard_map.105.source), channel_id=1, source_target_pairs={{0,16},{16,32},{32,48},{48,64},{64,80},{80,96},{96,112},{112,128},... | collective-permute-start | bytes 1769480 | tf_op jit(solution)/shard_map/ppermute | solution.py:299
  26.3 11.2 %collective-permute-start.4 = (bf16[2,384,384]{2,1,0:T(8,128)(2,1)S(1)}, bf16[2,384,384]{2,1,0:T(8,128)(2,1)S(1)}, u32[]{:S(2)}, u32[]{:S(2)}) collective-permute-start(bf16[2,384,384]{2,1,0:T(8,128)(2,1)S(1)} %get-tuple-element.33), channel_id=1, source_target_pairs={{0,16},{16,32},{32,48},{48,64},{64,80},{80,96},{96,112},{112,128},... | collective-permute-start | bytes 1769480 | tf_op jit(solution)/shard_map/ppermute | solution.py:299

commit v3 on v2

--- a/solution.py
+++ b/solution.py
@@ -56,7 +56,6 @@
         copy.start()
     for copy in copies[:3]:
         copy.wait()
-    spectrum[...] = to_spectrum(start[...].reshape(tall.shape), basis, basis_t, wide)
     lateral = detail.shape[0]
     blocks = lateral // BLOCK
     half = lateral // 2
@@ -104,16 +103,12 @@
 
     rows = 32
 
-    def spectral(index, carry):
-        start = pl.multiple_of(index * rows, rows)
-        real, imag = phases(start, rows)
-        for first in (0, half):
-            here = pl.ds(pl.multiple_of(start + first, rows), rows)
+    spectrum[...] = to_spectrum(start[...].reshape(tall.shape), basis, basis_t, wide)
+    for first in range(0, half, rows):
+        real, imag = phases(first, rows)
+        for here in (slice(first, first + rows), slice(half + first, half + first + rows)):
             phase_re[here, :] = real
             phase_im[here, :] = imag
-        return carry
-
-    lax.fori_loop(0, half // rows, spectral, 0, unroll=2)
     phase_re[half : half + 8, :], phase_im[half : half + 8, :] = phases(half, 8)
     for first in range(0, lateral, rows):
         here = slice(first, first + rows)

time: 77 us -> 76 us (0.987)
  Pallas kernels: 19.3 us -> 18.3 us
    pallas_call x1, Pallas kernels: 4.98 us -> 3.95 us  [per_device(): call(opening_body, [pl.BlockSpec(memory_space=pltpu.SMEM)] + [pl.BlockSpe...]
  transfers between devices with their start and end apart: 5 -> 5, of which waited for: 3 -> 3; matrix products, arithmetic and copies ran while one was open for 0% -> 0% of each run, Pallas kernels for 11% -> 12%
where the time goes in v3:
time: 76 us; the launch traced here: 75.7 us
  blocking collectives  33.5 us (44%)
  Pallas kernels  18.3 us (24%)
  starting transfers between devices  15.9 us (21%)
  waiting for transfers between devices  6.52 us (9%)
  between operations  1.4 us (2%)
    all_to_all x2, blocking collectives, exchanged(): lax.all_to_all(parcel, 'freq', split_axis=0, concat_axis=0, tiled=True)  33.5 us
    ppermute x5, starting transfers between devices, passed_along(): return lax.ppermute(block, axis, route)  15.9 us
    ppermute x5, waiting for transfers between devices, passed_along(): return lax.ppermute(block, axis, route)  6.52 us
    pallas_call x2, Pallas kernels, per_device(): call(partial(last_source_body if last else later_body, tick), [vmem] * le...  4.31 us
    pallas_call x1, Pallas kernels, per_device(): call(opening_body, [pl.BlockSpec(memory_space=pltpu.SMEM)] + [pl.BlockSpe...  3.95 us
    pallas_call x1, Pallas kernels, per_device(): call(upward_body, [vmem] * (3 + TABLES), [jax.ShapeDtypeStruct((rows, n),...  2.98 us
    pallas_call x1, Pallas kernels, per_device(): call(partial(last_image_body, TICKS - 1), [vmem] * len(args), parcel_shap...  2.37 us
    pallas_call x1, Pallas kernels, per_device(): call(partial(later_image_body, tick), [vmem] * len(args), [field, cells,...  2.25 us
  transfers between devices with their start and end apart: 5, of which 3 were waited for; matrix products, arithmetic and copies ran while one was open for 0% of the time, Pallas kernels for 12%

profile of v3, /device:TPU:96, one launch (start us, length us, event | category | flops | bytes accessed | tf_op | source)
XLA Modules:
  0.0 75.7 jit_solution(5272407912156876292)
XLA Ops:
  1.3 4.0 %shard_map.104 = (bf16[384,384]{1,0:T(8,128)(2,1)S(1)}, bf16[384,384]{1,0:T(8,128)(2,1)S(1)}, f32[384,384]{1,0:T(8,128)S(1)}, f32[384,384]{1,0:T(8,128)S(1)}, f3...) custom-call(f32[1]{0:T(128)S(6)} %copy.13.angular, ...), custom_call_target="tpu_custom_call" | custom-call | flops 905969664 | bytes 1179648 | tf_op jit(solution)/shard_map/pallas_call | solution.py:333
  5.2 0.0 copy-start.1
  5.2 0.0 copy-start
  5.3 2.2 %collective-permute-start = (bf16[2,384,384]{2,1,0:T(8,128)(2,1)S(1)}, bf16[2,384,384]{2,1,0:T(8,128)(2,1)S(1)}, u32[]{:S(2)}, u32[]{:S(2)}) collective-permute-start(bf16[2,384,384]{2,1,0:T(8,128)(2,1)S(1)} %get-tuple-element.20.source), channel_id=1, source_target_pairs={{0,16},{16,32},{32,48},{48,64},{64,80},{80,96},{96,112},{112,128},... | collective-permute-start | bytes 1769480 | tf_op jit(solution)/shard_map/ppermute | solution.py:294
  7.5 2.1 %shard_map.106 = (bf16[2,384,384]{2,1,0:T(8,128)(2,1)S(1)}, f32[384,384]{1,0:T(8,128)S(1)}, f32[384,384]{1,0:T(8,128)S(1)}) custom-call(bf16[2,384,384]{2,1,0:T(8,128)(2,1)S(1)} %get-tuple-element.27.start, bf16[2,384,384]{2,1,0:T(8,128)(2,1)S(1)} %get-tuple-element.20.source, bf16[384,384]{1,0:T(8,128)(2,1)S(1)} %get-tuple-element.21.refs_0_, ...), custom_call_target="tpu_custom_call" | custom-call | flops 905969664 | bytes 1179648 | tf_op jit(solution)/shard_map/pallas_call | solution.py:340
  9.6 5.1 %collective-permute-start.2 = (bf16[2,384,384]{2,1,0:T(8,128)(2,1)S(1)}, bf16[2,384,384]{2,1,0:T(8,128)(2,1)S(1)}, u32[]{:S(2)}, u32[]{:S(2)}) collective-permute-start(bf16[2,384,384]{2,1,0:T(8,128)(2,1)S(1)} %get-tuple-element.28), channel_id=1, source_target_pairs={{0,16},{16,32},{32,48},{48,64},{64,80},{80,96},{96,112},{112,128},... | collective-permute-start | bytes 1769480 | tf_op jit(solution)/shard_map/ppermute | solution.py:294
  14.8 0.0 copy-done.1
  14.8 1.9 %collective-permute-start.3 = (bf16[2,384,384]{2,1,0:T(8,128)(2,1)S(1)}, bf16[2,384,384]{2,1,0:T(8,128)(2,1)S(1)}, u32[]{:S(2)}, u32[]{:S(2)}) collective-permute-start(bf16[2,384,384]{2,1,0:T(8,128)(2,1)S(1)} %bitcast.7), channel_id=1, source_target_pairs={{16,0},{32,16},{48,32},{64,48},{80,64},{96,80},{112,96},{128,112},... | collective-permute-start | bytes 1769480 | tf_op jit(solution)/shard_map/ppermute | solution.py:294
  16.7 0.0 collective-permute-done.arrived
  16.7 0.0 copy-done
  16.7 2.0 %shard_map.105.source = bf16[2,384,384]{2,1,0:T(8,128)(2,1)S(1)} custom-call(bf16[2,384,384]{2,1,0:T(8,128)(2,1)S(1)} %collective-permute-done.arrived, bf16[2,2,1,2,384,384]{5,4,3,2,1,0:T(8,128)(2,1)S(1)} %copy-done, bf16[384,384]{1,0:T(8,128)(2,1)S(1)} %get-tuple-element.21.refs_0_, bf16[384,384]{1,0:T(8,128)(2,1)S(1)} %get-tuple-element.22.refs_1_, ...), custom_call_target="tpu_custom_call" | custom-call | flops 905969664 | bytes 1179648 | tf_op jit(solution)/shard_map/pallas_call | solution.py:349
  18.7 2.7 %collective-permute-start.1 = (bf16[2,384,384]{2,1,0:T(8,128)(2,1)S(1)}, bf16[2,384,384]{2,1,0:T(8,128)(2,1)S(1)}, u32[]{:S(2)}, u32[]{:S(2)}) collective-permute-start(bf16[2,384,384]{2,1,0:T(8,128)(2,1)S(1)} %shard_map.105.source), channel_id=1, source_target_pairs={{0,16},{16,32},{32,48},{48,64},{64,80},{80,96},{96,112},{112,128},... | collective-permute-start | bytes 1769480 | tf_op jit(solution)/shard_map/ppermute | solution.py:294
  21.4 1.6 %collective-permute-done.2.arrived = bf16[2,384,384]{2,1,0:T(8,128)(2,1)S(1)} collective-permute-done((bf16[2,384,384]{2,1,0:T(8,128)(2,1)S(1)}, bf16[2,384,384]{2,1,0:T(8,128)(2,1)S(1)}, u32[]{:S(2)}, u32[]{:S(2)}) %collective-permute-start.2) | collective-permute-done | bytes 589856 | tf_op jit(solution)/shard_map/ppermute | solution.py:294
  23.0 2.2 %shard_map.107 = (bf16[2,384,384]{2,1,0:T(8,128)(2,1)S(1)}, f32[384,384]{1,0:T(8,128)S(1)}, f32[384,384]{1,0:T(8,128)S(1)}) custom-call(bf16[2,384,384]{2,1,0:T(8,128)(2,1)S(1)} %collective-permute-done.2.arrived, bf16[2,2,1,2,384,384]{5,4,3,2,1,0:T(8,128)(2,1)S(1)} %copy-done, bf16[2,384,384]{2,1,0:T(8,128)(2,1)S(1)} %shard_map.105.source, ...), custom_call_target="tpu_custom_call" | custom-call | flops 905969664 | bytes 1179648 | tf_op jit(solution)/shard_map/pallas_call | solution.py:360
  25.3 4.0 %collective-permute-start.4 = (bf16[2,384,384]{2,1,0:T(8,128)(2,1)S(1)}, bf16[2,384,384]{2,1,0:T(8,128)(2,1)S(1)}, u32[]{:S(2)}, u32[]{:S(2)}) collective-permute-start(bf16[2,384,384]{2,1,0:T(8,128)(2,1)S(1)} %get-tuple-element.33), channel_id=1, source_target_pairs={{0,16},{16,32},{32,48},{48,64},{64,80},{80,96},{96,112},{112,128},... | collective-permute-start | bytes 1769480 | tf_op jit(solution)/shard_map/ppermute | solution.py:294
  29.3 0.6 collective-permute-done.1.arrived
  29.9 2.3 %shard_map.108 = (bf16[2,384,384]{2,1,0:T(8,128)(2,1)S(1)}, bf16[16,160,128]{2,1,0:T(8,128)(2,1)S(1)}) custom-call(bf16[2,384,384]{2,1,0:T(8,128)(2,1)S(1)} %collective-permute-done.1.arrived, bf16[2,2,1,2,384,384]{5,4,3,2,1,0:T(8,128)(2,1)S(1)} %copy-done, f32[384,384]{1,0:T(8,128)S(1)} %get-tuple-element.31.illum_in, ...), custom_call_target="tpu_custom_call" | custom-call | flops 905969664 | bytes 1179648 | tf_op jit(solution)/shard_map/pallas_call | solution.py:349
  32.3 0.0 collective-permute-done.3.rising
  32.3 4.2 %collective-permute-done.4.arrived = bf16[2,384,384]{2,1,0:T(8,128)(2,1)S(1)} collective-permute-done((bf16[2,384,384]{2,1,0:T(8,128)(2,1)S(1)}, bf16[2,384,384]{2,1,0:T(8,128)(2,1)S(1)}, u32[]{:S(2)}, u32[]{:S(2)}) %collective-permute-start.4) | collective-permute-done | bytes 589856 | tf_op jit(solution)/shard_map/ppermute | solution.py:294
  36.5 2.4 %shard_map.109 = bf16[16,160,128]{2,1,0:T(8,128)(2,1)S(1)} custom-call(bf16[16,160,128]{2,1,0:T(8,128)(2,1)S(1)} %get-tuple-element.32.begun, bf16[2,384,384]{2,1,0:T(8,128)(2,1)S(1)} %collective-permute-done.3.rising, bf16[2,384,384]{2,1,0:T(8,128)(2,1)S(1)} %collective-permute-done.4.arrived, ...), custom_call_target="tpu_custom_call", output_to_operand_aliasing={{}: (0, {})} | custom-call | flops 905969664 | bytes 1179648 | tf_op jit(solution)/shard_map/pallas_call | solution.py:364
  38.9 20.1 %all_to_all.10.parcel = bf16[16,160,128]{2,1,0:T(8,128)(2,1)S(1)} all-to-all(bf16[16,160,128]{2,1,0:T(8,128)(2,1)S(1)} %shard_map.109), channel_id=1, replica_groups=mesh['depth'=16,'freq'=16] {'freq'}, dimensions={0} | all-to-all | bytes 1310720 | tf_op jit(solution)/shard_map/all_to_all | solution.py:298
  58.9 0.3 shard_map.110
  59.2 13.5 %all_to_all.11.parcel = bf16[16,80,128]{2,1,0:T(8,128)(2,1)S(1)} all-to-all(bf16[16,80,128]{2,1,0:T(8,128)(2,1)S(1)} %shard_map.110), channel_id=1, replica_groups=mesh['depth'=16,'freq'=16] {'freq'}, dimensions={0} | all-to-all | bytes 655360 | tf_op jit(solution)/shard_map/all_to_all | solution.py:298
  72.7 3.0 %shard_map.111 = (bf16[24,384]{1,0:T(8,128)(2,1)}, bf16[2,384,384]{2,1,0:T(8,128)(2,1)}) custom-call(bf16[16,80,128]{2,1,0:T(8,128)(2,1)S(1)} %all_to_all.11.parcel, bf16[2,384,384]{2,1,0:T(8,128)(2,1)S(1)} %collective-permute-done.3.rising, bf16[2,384,384]{2,1,0:T(8,128)(2,1)S(1)} %get-tuple-element.34.source, ...), custom_call_target="tpu_custom_call" | custom-call | flops 905969664 | bytes 1179648 | tf_op jit(solution)/shard_map/pallas_call | solution.py:373
Async XLA Ops:
  5.2 9.5 %copy-start.1 = (bf16[1,1,2,384,384]{4,3,2,1,0:T(8,128)(2,1)S(1)}, bf16[1,1,2,384,384]{4,3,2,1,0:T(8,128)(2,1)}, u32[]{:S(2)}) copy-start(bf16[1,1,2,384,384]{4,3,2,1,0:T(8,128)(2,1)} %param.11) | copy-start | bytes 1769476
  5.2 11.5 %copy-start = (bf16[2,2,1,2,384,384]{5,4,3,2,1,0:T(8,128)(2,1)S(1)}, bf16[2,2,1,2,384,384]{5,4,3,2,1,0:T(8,128)(2,1)}, u32[]{:S(2)}) copy-start(bf16[2,2,1,2,384,384]{5,4,3,2,1,0:T(8,128)(2,1)} %surface.7) | copy-start | bytes 7077892
  5.3 11.5 %collective-permute-start = (bf16[2,384,384]{2,1,0:T(8,128)(2,1)S(1)}, bf16[2,384,384]{2,1,0:T(8,128)(2,1)S(1)}, u32[]{:S(2)}, u32[]{:S(2)}) collective-permute-start(bf16[2,384,384]{2,1,0:T(8,128)(2,1)S(1)} %get-tuple-element.20.source), channel_id=1, source_target_pairs={{0,16},{16,32},{32,48},{48,64},{64,80},{80,96},{96,112},{112,128},... | collective-permute-start | bytes 1769480 | tf_op jit(solution)/shard_map/ppermute | solution.py:294
  9.6 13.4 %collective-permute-start.2 = (bf16[2,384,384]{2,1,0:T(8,128)(2,1)S(1)}, bf16[2,384,384]{2,1,0:T(8,128)(2,1)S(1)}, u32[]{:S(2)}, u32[]{:S(2)}) collective-permute-start(bf16[2,384,384]{2,1,0:T(8,128)(2,1)S(1)} %get-tuple-element.28), channel_id=1, source_target_pairs={{0,16},{16,32},{32,48},{48,64},{64,80},{80,96},{96,112},{112,128},... | collective-permute-start | bytes 1769480 | tf_op jit(solution)/shard_map/ppermute | solution.py:294
  14.8 17.5 %collective-permute-start.3 = (bf16[2,384,384]{2,1,0:T(8,128)(2,1)S(1)}, bf16[2,384,384]{2,1,0:T(8,128)(2,1)S(1)}, u32[]{:S(2)}, u32[]{:S(2)}) collective-permute-start(bf16[2,384,384]{2,1,0:T(8,128)(2,1)S(1)} %bitcast.7), channel_id=1, source_target_pairs={{16,0},{32,16},{48,32},{64,48},{80,64},{96,80},{112,96},{128,112},... | collective-permute-start | bytes 1769480 | tf_op jit(solution)/shard_map/ppermute | solution.py:294
  18.7 11.2 %collective-permute-start.1 = (bf16[2,384,384]{2,1,0:T(8,128)(2,1)S(1)}, bf16[2,384,384]{2,1,0:T(8,128)(2,1)S(1)}, u32[]{:S(2)}, u32[]{:S(2)}) collective-permute-start(bf16[2,384,384]{2,1,0:T(8,128)(2,1)S(1)} %shard_map.105.source), channel_id=1, source_target_pairs={{0,16},{16,32},{32,48},{48,64},{64,80},{80,96},{96,112},{112,128},... | collective-permute-start | bytes 1769480 | tf_op jit(solution)/shard_map/ppermute | solution.py:294
  25.3 11.2 %collective-permute-start.4 = (bf16[2,384,384]{2,1,0:T(8,128)(2,1)S(1)}, bf16[2,384,384]{2,1,0:T(8,128)(2,1)S(1)}, u32[]{:S(2)}, u32[]{:S(2)}) collective-permute-start(bf16[2,384,384]{2,1,0:T(8,128)(2,1)S(1)} %get-tuple-element.33), channel_id=1, source_target_pairs={{0,16},{16,32},{32,48},{48,64},{64,80},{80,96},{96,112},{112,128},... | collective-permute-start | bytes 1769480 | tf_op jit(solution)/shard_map/ppermute | solution.py:294
